TPU v7x, 256 devices: a whole 4x4x8 slice. The times are simulated.
256 devices in a mesh: unit: 4 (over y_lo, core), zero: 32 (over z, y_hi, x_hi), cols: 2 (over x_lo).
Axes of the slice: x: 4 (x_hi: 2, x_lo: 2; x = x_hi * 2 + x_lo), y: 4 (y_hi: 2, y_lo: 2; y = y_hi * 2 + y_lo), z: 8, core: 2. Of those that a mesh axis runs over, the one named last changes fastest.
Arguments:
- weight_gate: bfloat16 [20480, 13824], P(('unit', 'zero'), 'cols'), parts along dimension 0, may hold values from -0.15625 to 0.15625
- low_gate: bfloat16 [20480, 32], P(('unit', 'zero')), parts along dimension 0, may hold values from -0.078125 to 0.078125
- high_gate: bfloat16 [128, 13824], P('unit', 'cols'), parts along dimension 0, may hold values from -1 to 1
- weight_up: bfloat16 [20480, 13824], P(('unit', 'zero'), 'cols'), parts along dimension 0, may hold values from -0.15625 to 0.15625
- low_up: bfloat16 [20480, 32], P(('unit', 'zero')), parts along dimension 0, may hold values from -0.078125 to 0.078125
- high_up: bfloat16 [128, 13824], P('unit', 'cols'), parts along dimension 0, may hold values from -1 to 1
- norm_train: float32 [20480], P(('unit', 'zero', 'cols')), parts along dimension 0, may hold values from 0.25 to 1.75
- norm_step: float32 [20480], P(('unit', 'zero', 'cols')), parts along dimension 0, may hold values from -0.3 to 0.3
Outputs:
- final_gate: bfloat16 [20480, 13824], P('unit', ('cols', 'zero')), parts along dimension 0
- final_up: bfloat16 [20480, 13824], P('unit', ('cols', 'zero')), parts along dimension 0
- scale_gate: float32 [55296], P(('unit', 'cols', 'zero')), parts along dimension 0
- scale_up: float32 [55296], P(('unit', 'cols', 'zero')), parts along dimension 0
- serve_norm: bfloat16 [20480], P('unit'), parts along dimension 0
There are 4 independent parts, one for each index of `unit`. A program takes and returns all parts, laid end to end along the dimension named above; each array names one. Nothing has to cross between parts.
All inputs are finite; a program needn't handle non-finite values. Where the computation divides by a largest or mean magnitude, that divisor is 1e-20 or more.
Results may differ from a plain program's by a relative error of at most 0.001.
Values may be sent and summed in bfloat16 or wider, within the bound.
No kernel may reach another device: no remote copies, remote signals or barrier semaphores. Data moves between devices by JAX's collectives and lax.ppermute only.
A program may use at most 128 MiB of HBM per device.

v0:
```python
import jax
import jax.numpy as jnp
from jax import lax
from jax.sharding import PartitionSpec as P

D_MODEL = 5120


mix_rate = 0.5


def copy_for_each(value, axis):
    copies = jnp.broadcast_to(value, (lax.axis_size(axis), *value.shape))
    return lax.all_to_all(copies, axis, split_axis=0, concat_axis=0, tiled=True)


def over_copies(value, axis):
    return copy_for_each(value, axis).sum(axis=0)


def together(arrays, axis):
    vector, at, outs = (jnp.concatenate([a.reshape(-1) for a in arrays]), 0, [])
    total = over_copies(vector, axis)
    for a in arrays:
        outs.append(total[at : at + a.size].reshape(a.shape))
        at += a.size
    return tuple(outs)


def laid_out(blocks, dim):
    blocks = jnp.moveaxis(blocks, 0, dim)
    dims = blocks.shape
    return blocks.reshape(*dims[:dim], dims[dim] * dims[dim + 1], *dims[dim + 2 :])


def gathered_copies(value, axis, dim):
    return laid_out(copy_for_each(value, axis), dim)


def local(weight_gate, low_gate, high_gate, weight_up, low_up, high_up, norm_train, norm_step):
    result_gate = weight_gate.astype(jnp.float32) + mix_rate * jnp.dot(
        low_gate, high_gate, preferred_element_type=jnp.float32
    )
    result_up = weight_up.astype(jnp.float32) + mix_rate * jnp.dot(
        low_up, high_up, preferred_element_type=jnp.float32
    )
    total_gate, total_up = together(
        (jnp.sum(jnp.abs(result_gate), axis=0), jnp.sum(jnp.abs(result_up), axis=0)), "zero"
    )
    scale_gate = total_gate / D_MODEL
    scale_up = total_up / D_MODEL
    narrow_gate, narrow_up = (
        (result_gate / scale_gate).astype(jnp.bfloat16),
        (result_up / scale_up).astype(jnp.bfloat16),
    )
    final_gate, final_up = (
        lax.all_to_all(narrow_gate, "zero", split_axis=1, concat_axis=0, tiled=True),
        lax.all_to_all(narrow_up, "zero", split_axis=1, concat_axis=0, tiled=True),
    )
    place = lax.axis_index("zero")
    scale_gate = lax.dynamic_slice_in_dim(
        scale_gate, place * final_gate.shape[1], final_gate.shape[1]
    )
    scale_up = lax.dynamic_slice_in_dim(scale_up, place * final_up.shape[1], final_up.shape[1])
    serve_norm = gathered_copies((norm_train + norm_step).astype(jnp.bfloat16), ("zero", "cols"), 0)
    return (final_gate, final_up, scale_gate, scale_up, serve_norm)


def solution(mesh):
    in_specs = (
        P(("unit", "zero"), "cols"),
        P(("unit", "zero"), None),
        P("unit", "cols"),
        P(("unit", "zero"), "cols"),
        P(("unit", "zero"), None),
        P("unit", "cols"),
        P(("unit", "zero", "cols")),
        P(("unit", "zero", "cols")),
    )
    out_specs = (
        P("unit", ("cols", "zero")),
        P("unit", ("cols", "zero")),
        P(("unit", "cols", "zero")),
        P(("unit", "cols", "zero")),
        P("unit"),
    )
    return jax.shard_map(local, mesh=mesh, in_specs=in_specs, out_specs=out_specs, check_vma=False)
```

profile of v0, /device:TPU:6, one launch (start us, length us, event | category | flops | bytes accessed | tf_op | source)
XLA Modules:
  0.0 240.7 jit_solution(5626973775937074867)
XLA Ops:
  0.6 0.0 copy-start
  0.6 0.0 copy-start.2
  0.7 0.0 copy-start.1
  0.7 0.0 copy-start.3
  0.7 1.0 copy-done
  1.7 4.7 %abs_reduce_fusion = (f32[6912]{0:T(1024)S(1)}, f32[160,6912]{1,0:T(8,128)}) fusion(bf16[160,32]{0,1:T(8,128)(2,1)} %param.12, bf16[32,6912]{1,0:T(8,128)(2,1)S(1)} %copy-done, bf16[160,6912]{1,0:T(8,128)(2,1)} %param.11), kind=kOutput, calls=%fused_computation.6 | convolution fusion | flops 76301568 | bytes 7115776 | tf_op jit(solution)/shard_map/dot_general | solution.py:44
  6.3 0.0 copy-done.1
  6.3 3.1 %abs_reduce_fusion.1 = (f32[6912]{0:T(1024)S(1)}, f32[160,6912]{1,0:T(8,128)}) fusion(bf16[160,32]{0,1:T(8,128)(2,1)S(1)} %copy-done.3, bf16[32,6912]{1,0:T(8,128)(2,1)S(1)} %copy-done.2, bf16[160,6912]{1,0:T(8,128)(2,1)S(1)} %copy-done.1), kind=kOutput, calls=%fused_computation.7 | convolution fusion | flops 76301568 | bytes 7115776 | tf_op jit(solution)/shard_map/dot_general | solution.py:41
  9.4 2.1 broadcast_in_dim.8
  11.6 14.2 %all-to-all-start = ((f32[32,1,13824]{2,1,0:T(1,128)}), f32[32,1,13824]{2,1,0:T(1,128)S(1)}, u32[]{:S(2)}, u32[]{:S(2)}) async-start(f32[32,1,13824]{2,1,0:T(1,128)} %broadcast_in_dim.8), calls=%async_computation | async-start | bytes 3538944 | tf_op jit(solution)/shard_map/all_to_all | solution.py:14
  25.8 0.0 copy-done.4
  25.8 0.0 copy-done.5
  25.8 42.4 %all-to-all-done = f32[32,1,13824]{2,1,0:T(1,128)S(1)} async-done(((f32[32,1,13824]{2,1,0:T(1,128)}), f32[32,1,13824]{2,1,0:T(1,128)S(1)}, u32[]{:S(2)}, u32[]{:S(2)}) %all-to-all-start) | async-done | bytes 1769504 | tf_op jit(solution)/shard_map/all_to_all | solution.py:14
  68.2 0.6 broadcast_in_dim.9
  68.9 8.9 %all-to-all-start.3 = ((bf16[64,1,80]{2,1,0:T(2,128)(2,1)}), bf16[64,1,80]{2,1,0:T(2,128)(2,1)S(1)}, u32[]{:S(2)}, u32[]{:S(2)}) async-start(bf16[64,1,80]{2,1,0:T(2,128)(2,1)} %broadcast_in_dim.9), calls=%async_computation.3 | async-start | bytes 65536 | tf_op jit(solution)/shard_map/all_to_all | solution.py:14
  77.7 1.0 reduce_sum.29
  78.7 6.2 %divide_convert_fusion = (bf16[160,6912]{1,0:T(8,128)(2,1)}, bf16[160,6912]{1,0:T(8,128)(2,1)}) fusion(f32[160,6912]{1,0:T(8,128)} %get-tuple-element.28, f32[6912]{0:T(1024)S(1)} %get-tuple-element.25, f32[160,6912]{1,0:T(8,128)} %get-tuple-element.30, f32[6912]{0:T(1024)S(1)} %get-tuple-element.26), kind=kLoop, calls=%fused_computation.4 | loop fusion | flops 4423680 | bytes 13326336 | tf_op jit(solution)/shard_map/convert_element_type | solution.py:54
  85.0 9.0 %all_to_all.37 = bf16[160,32,216]{2,1,0:T(8,128)(2,1)S(1)} reshape(bf16[160,6912]{1,0:T(8,128)(2,1)} %get-tuple-element.32) | data formatting | bytes 4423680 | tf_op jit(solution)/shard_map/all_to_all | solution.py:57
  94.0 3.0 %copy.28 = bf16[160,32,216]{2,0,1:T(8,128)(2,1)} copy(bf16[160,32,216]{2,1,0:T(8,128)(2,1)S(1)} %all_to_all.37) | data formatting | bytes 4423680 | tf_op jit(solution)/shard_map/all_to_all | solution.py:57
  97.0 0.0 all-to-all-done.3
  97.0 12.3 %all-to-all-start.1 = ((bf16[160,32,216]{2,0,1:T(8,128)(2,1)}), bf16[160,32,216]{2,0,1:T(8,128)(2,1)S(1)}, u32[]{:S(2)}, u32[]{:S(2)}) async-start(bf16[160,32,216]{2,0,1:T(8,128)(2,1)} %copy.28), calls=%async_computation.1 | async-start | bytes 5242880 | tf_op jit(solution)/shard_map/all_to_all | solution.py:57
  109.4 9.9 %all_to_all.41 = bf16[160,32,216]{2,1,0:T(8,128)(2,1)} reshape(bf16[160,6912]{1,0:T(8,128)(2,1)} %get-tuple-element.31) | data formatting | bytes 4423680 | tf_op jit(solution)/shard_map/all_to_all | solution.py:58
  119.2 4.7 %copy.29 = bf16[160,32,216]{2,0,1:T(8,128)(2,1)} copy(bf16[160,32,216]{2,1,0:T(8,128)(2,1)} %all_to_all.41) | data formatting | bytes 4423680 | tf_op jit(solution)/shard_map/all_to_all | solution.py:58
  123.9 44.4 %all-to-all-done.1 = bf16[160,32,216]{2,0,1:T(8,128)(2,1)S(1)} async-done(((bf16[160,32,216]{2,0,1:T(8,128)(2,1)}), bf16[160,32,216]{2,0,1:T(8,128)(2,1)S(1)}, u32[]{:S(2)}, u32[]{:S(2)}) %all-to-all-start.1) | async-done | bytes 2211872 | tf_op jit(solution)/shard_map/all_to_all | solution.py:57
  168.3 9.0 %all-to-all-start.2 = ((bf16[160,32,216]{2,0,1:T(8,128)(2,1)}), bf16[160,32,216]{2,0,1:T(8,128)(2,1)}, u32[]{:S(2)}, u32[]{:S(2)}) async-start(bf16[160,32,216]{2,0,1:T(8,128)(2,1)} %copy.29), calls=%async_computation.2 | async-start | bytes 5242880 | tf_op jit(solution)/shard_map/all_to_all | solution.py:58
  177.4 0.1 reduce.1
  177.5 0.7 reshape.30
  178.2 0.6 dynamic_slice.6
  178.8 0.6 dynamic_slice.7
  179.4 2.5 %copy.30 = bf16[5120,216]{0,1:T(8,128)(2,1)} copy(bf16[5120,216]{1,0:T(8,128)(2,1)S(1)} %bitcast.10) | data formatting | bytes 4423680
  181.9 54.5 %all-to-all-done.2 = bf16[160,32,216]{2,0,1:T(8,128)(2,1)} async-done(((bf16[160,32,216]{2,0,1:T(8,128)(2,1)}), bf16[160,32,216]{2,0,1:T(8,128)(2,1)}, u32[]{:S(2)}, u32[]{:S(2)}) %all-to-all-start.2) | async-done | bytes 2211872 | tf_op jit(solution)/shard_map/all_to_all | solution.py:58
  236.4 4.3 %copy.31 = bf16[5120,216]{0,1:T(8,128)(2,1)} copy(bf16[5120,216]{1,0:T(8,128)(2,1)} %bitcast.3) | data formatting | bytes 4423680
  (7 shorter events, 0.0 us)
Async XLA Ops:
  0.6 1.0 copy-start
  0.6 5.7 %copy-start.2 = (bf16[32,6912]{1,0:T(8,128)(2,1)S(1)}, bf16[32,6912]{1,0:T(8,128)(2,1)}, u32[]{:S(2)}) copy-start(bf16[32,6912]{1,0:T(8,128)(2,1)} %param.10) | copy-start | bytes 1327108
  0.7 5.7 %copy-start.1 = (bf16[160,6912]{1,0:T(8,128)(2,1)S(1)}, bf16[160,6912]{1,0:T(8,128)(2,1)}, u32[]{:S(2)}) copy-start(bf16[160,6912]{1,0:T(8,128)(2,1)} %param.8) | copy-start | bytes 6635524
  0.7 5.7 %copy-start.3 = (bf16[160,32]{0,1:T(8,128)(2,1)S(1)}, bf16[160,32]{0,1:T(8,128)(2,1)}, u32[]{:S(2)}) copy-start(bf16[160,32]{0,1:T(8,128)(2,1)} %param.9) | copy-start | bytes 30724
  9.4 16.4 %copy-start.4 = (f32[80]{0:T(128)S(1)}, f32[80]{0:T(128)}, u32[]{:S(2)}) copy-start(f32[80]{0:T(128)} %param.14) | copy-start | bytes 964
  9.4 16.4 %copy-start.5 = (f32[80]{0:T(128)S(1)}, f32[80]{0:T(128)}, u32[]{:S(2)}) copy-start(f32[80]{0:T(128)} %param.15) | copy-start | bytes 964
  11.6 56.7 %all-to-all-start = ((f32[32,1,13824]{2,1,0:T(1,128)}), f32[32,1,13824]{2,1,0:T(1,128)S(1)}, u32[]{:S(2)}, u32[]{:S(2)}) async-start(f32[32,1,13824]{2,1,0:T(1,128)} %broadcast_in_dim.8), calls=%async_computation | async-start | bytes 3538944 | tf_op jit(solution)/shard_map/all_to_all | solution.py:14
  68.9 28.2 %all-to-all-start.3 = ((bf16[64,1,80]{2,1,0:T(2,128)(2,1)}), bf16[64,1,80]{2,1,0:T(2,128)(2,1)S(1)}, u32[]{:S(2)}, u32[]{:S(2)}) async-start(bf16[64,1,80]{2,1,0:T(2,128)(2,1)} %broadcast_in_dim.9), calls=%async_computation.3 | async-start | bytes 65536 | tf_op jit(solution)/shard_map/all_to_all | solution.py:14
  97.0 71.3 %all-to-all-start.1 = ((bf16[160,32,216]{2,0,1:T(8,128)(2,1)}), bf16[160,32,216]{2,0,1:T(8,128)(2,1)S(1)}, u32[]{:S(2)}, u32[]{:S(2)}) async-start(bf16[160,32,216]{2,0,1:T(8,128)(2,1)} %copy.28), calls=%async_computation.1 | async-start | bytes 5242880 | tf_op jit(solution)/shard_map/all_to_all | solution.py:57
  168.3 68.1 %all-to-all-start.2 = ((bf16[160,32,216]{2,0,1:T(8,128)(2,1)}), bf16[160,32,216]{2,0,1:T(8,128)(2,1)}, u32[]{:S(2)}, u32[]{:S(2)}) async-start(bf16[160,32,216]{2,0,1:T(8,128)(2,1)} %copy.29), calls=%async_computation.2 | async-start | bytes 5242880 | tf_op jit(solution)/shard_map/all_to_all | solution.py:58
where the time goes:
time: 245 us; the launch traced here: 241 us
  waiting for transfers between devices  141 us (58%)
  starting transfers between devices  44.4 us (18%)
  local copies, waits for them, and re-layouts  39.1 us (16%)
  matrix products  7.77 us (3%)
  other arithmetic  7.35 us (3%)
    all_to_all x1, waiting for transfers between devices, local(): lax.all_to_all(narrow_up, 'zero', split_axis=1, concat_axis=0, tiled=True)  54.5 us
    all_to_all x1, waiting for transfers between devices, local(): lax.all_to_all(narrow_gate, 'zero', split_axis=1, concat_axis=0, tiled=True)  44.4 us
    all_to_all x2, waiting for transfers between devices, copy_for_each(): return lax.all_to_all(copies, axis, split_axis=0, concat_axis=0, tiled=True)  42.4 us
    all_to_all x2, starting transfers between devices, copy_for_each(): return lax.all_to_all(copies, axis, split_axis=0, concat_axis=0, tiled=True)  23.1 us
    all_to_all x2, local copies, waits for them, and re-layouts, local(): lax.all_to_all(narrow_up, 'zero', split_axis=1, concat_axis=0, tiled=True)  14.6 us
    all_to_all x1, starting transfers between devices, local(): lax.all_to_all(narrow_gate, 'zero', split_axis=1, concat_axis=0, tiled=True)  12.3 us
    all_to_all x2, local copies, waits for them, and re-layouts, local(): lax.all_to_all(narrow_gate, 'zero', split_axis=1, concat_axis=0, tiled=True)  12 us
    all_to_all x1, starting transfers between devices, local(): lax.all_to_all(narrow_up, 'zero', split_axis=1, concat_axis=0, tiled=True)  9.02 us
  transfers between devices with their start and end apart: 4, of which 3 were waited for; matrix products, arithmetic and copies ran while one was open for 8% of the time, Pallas kernels for 0%

commit v1 on v0

v1 whole, which is shorter than its diff:
```python
import jax
import jax.numpy as jnp
from jax import lax
from jax.experimental import pallas as pl
from jax.experimental.pallas import tpu as pltpu
from jax.sharding import PartitionSpec as P

D_MODEL = 5120
MIX = 0.5
NZ = 8
NQ = 4
ROWS = 160
COLS = 216
RANK = 32
SPAN = NQ * COLS
TILES = 7
EXTRA = 48
BLOCK = TILES * ROWS + EXTRA
PART = 2 * ROWS + EXTRA
LAST = 51

Z_GROUPS = [[z * NQ + q for z in range(NZ)] for q in range(NQ)]
bf16, f32 = jnp.bfloat16, jnp.float32


def lanes(shape):
    return lax.broadcasted_iota(jnp.int32, shape, len(shape) - 1)


def rows(shape):
    return lax.broadcasted_iota(jnp.int32, shape, len(shape) - 2)


def place_t(low_t, period, first):
    shape = (RANK, 128)
    hit = (lanes(shape) >= first) & ((lanes(shape) - first) % period == rows(shape))
    return lax.dot_general(
        low_t, hit.astype(bf16), (((0,), (0,)), ((), ())), preferred_element_type=f32
    )


def pack_gate(weight, low_gate, low_up, train, step, out):
    wide = (ROWS, 128)
    low_g = place_t(low_gate[...], 128, 96)
    low_u = place_t(low_up[...], 32, 0)
    group = lanes((40, 128)) // 32
    packed = jnp.zeros((40, 128), f32)
    for g in range(4):
        packed = jnp.where(group == g, low_u[40 * g : 40 * g + 40], packed)
    norm = jnp.concatenate([train[...] + step[...], jnp.zeros((1, 48), f32)], axis=1)
    norm = jnp.broadcast_to(norm, (8, 128))
    extra = jnp.concatenate([packed, norm], axis=0).astype(bf16)
    for z in range(NZ):
        first, off = divmod(SPAN * z, 128)
        for j in range(TILES):
            t = first + j
            x = weight[:, 128 * t : 128 * t + 128].astype(f32)
            if off:
                x = pltpu.roll(x, 128 - off, 1)
                if j < TILES - 1 or off > 32:
                    y = weight[:, 128 * t + 128 : 128 * t + 256].astype(f32)
                    x = jnp.where(lanes(wide) < 128 - off, x, pltpu.roll(y, 128 - off, 1))
            if j == TILES - 1:
                x = jnp.where(lanes(wide) < 96, x, low_g)
            out[z, ROWS * j : ROWS * j + ROWS, :] = x.astype(bf16)
        out[z, ROWS * TILES : BLOCK, :] = extra


def window(x, off):
    return pltpu.roll(x, (384 - off) % 384, 1)[:, :256]


def pack_up(weight, high_gate, high_up, *outs):
    parts, mix, high = outs[:NQ], outs[NQ], outs[NQ + 1]
    place = lax.axis_index("zero")
    q = place % NQ
    for p in range(NQ):
        for z in range(NZ):
            start = COLS * (z * NQ + jnp.bitwise_xor(q, p))
            tile = jnp.minimum(start // 128, LAST)
            x = weight[:, pl.ds(pl.multiple_of(tile * 128, 128), 384)].astype(f32)
            x = window(x, start - 128 * tile).astype(bf16)
            parts[p][z, 0:ROWS, :] = x[:, :128]
            parts[p][z, ROWS : 2 * ROWS, :] = x[:, 128:]
    start = COLS * place
    tile = jnp.minimum(start // 128, LAST)
    at = pl.multiple_of(tile * 128, 128)

    def own(ref):
        x = pltpu.roll(ref[:, pl.ds(at, 384)].astype(f32), (384 - (start - 128 * tile)) % 384, 1)
        return x[:, :256].astype(bf16)

    def turned(h, first, width):
        shape = (RANK, width)
        hit = jnp.where(lanes(shape) == rows(shape) + first, MIX, 0.0).astype(bf16)
        return lax.dot_general(h, hit, (((0,), (0,)), ((), ())), preferred_element_type=f32)

    eye = (lanes((256, 256)) == rows((256, 256))) & (rows((256, 256)) < COLS)
    mix[...] = (eye.astype(f32) + turned(own(high_gate), COLS, 256)).astype(bf16)
    high[...] = turned(own(high_up), 0, 128).astype(bf16)


def turn_up(*refs):
    parts, out, x = refs[:NQ], refs[NQ], refs[NQ + 1]
    q = lax.axis_index("zero") % NQ
    eye = (lanes((COLS, 256)) == rows((COLS, 256))).astype(bf16)
    for z in range(NZ):
        for p in range(NQ):
            at = pl.multiple_of(jnp.bitwise_xor(q, p) * ROWS, ROWS)
            x[z % 2, pl.ds(at, ROWS), 0:128] = parts[p][z, 0:ROWS, :]
            x[z % 2, pl.ds(at, ROWS), 128:256] = parts[p][z, ROWS : 2 * ROWS, :]
        out[z] = lax.dot_general(
            eye, x[z % 2], (((1,), (1,)), ((), ())), preferred_element_type=f32
        ).astype(bf16)


def split_gate(block, *parts):
    q = lax.axis_index("zero") % NQ
    wide = (ROWS, 128)
    for z in range(NZ):
        low = pltpu.roll(block[z, ROWS * 6 : ROWS * 7, :].astype(f32), 120, 1)
        for p in range(NQ):
            start = COLS * jnp.bitwise_xor(q, p)
            tile = jnp.minimum(start // 128, TILES - 3)
            x = jnp.concatenate(
                [
                    block[z, pl.ds(pl.multiple_of((tile + k) * ROWS, ROWS), ROWS), :].astype(f32)
                    for k in range(3)
                ],
                axis=1,
            )
            x = window(x, start - 128 * tile)
            last = jnp.where(lanes(wide) < 88, x[:, 128:], jnp.where(lanes(wide) < 120, low, 0.0))
            parts[p][z, 0:ROWS, :] = x[:, :128].astype(bf16)
            parts[p][z, ROWS : 2 * ROWS, :] = last.astype(bf16)
            parts[p][z, 2 * ROWS : PART, :] = block[z, ROWS * TILES : BLOCK, :]


def scales(total):
    column = jnp.sum(total, axis=1, keepdims=True) / D_MODEL
    padded = jnp.concatenate([total, jnp.zeros((256 - COLS, 128), f32)], axis=0)
    row = jnp.sum(jnp.transpose(padded), axis=0, keepdims=True) / D_MODEL
    return column, row[:, :COLS]


def magnitudes(r):
    a = jnp.abs(r)
    return sum(a[:, 128 * k : 128 * k + 128] for k in range(5))


def last_gate(*refs):
    parts, mix = refs[:NQ], refs[NQ]
    out, scale, low, norm = refs[NQ + 1 : NQ + 5]
    x, lows, sums = refs[NQ + 5 :]
    q = lax.axis_index("zero") % NQ
    total = jnp.zeros((COLS, 128), f32)
    m = mix[0:COLS, :]
    pick = (lanes((RANK, 128)) == rows((RANK, 128))).astype(bf16)
    for z in range(NZ):
        for p in range(NQ):
            at = pl.multiple_of(jnp.bitwise_xor(q, p) * ROWS, ROWS)
            x[z % 2, pl.ds(at, ROWS), 0:128] = parts[p][z, 0:ROWS, :]
            x[z % 2, pl.ds(at, ROWS), 128:256] = parts[p][z, ROWS : 2 * ROWS, :]
            extra = parts[p][z, 2 * ROWS : PART, :].astype(f32)
            wide = jnp.concatenate(
                [pltpu.roll(extra[0:40], (128 - 32 * g) % 128, 1) for g in range(4)], axis=0
            )
            lows[z % 2, pl.ds(at, ROWS), :] = wide.astype(bf16)
            norm[z, pl.ds(jnp.bitwise_xor(q, p), 1), :] = extra[40:41]
        r = lax.dot_general(m, x[z % 2], (((1,), (1,)), ((), ())), preferred_element_type=f32)
        sums[:, 640 * z : 640 * z + 640] = r
        total = total + magnitudes(r)
        low[:, 640 * z : 640 * z + 640] = lax.dot_general(
            pick, lows[z % 2], (((1,), (1,)), ((), ())), preferred_element_type=f32
        ).astype(bf16)
    column, row = scales(total)
    scale[...] = row
    out[...] = (sums[...] * (1.0 / column)).astype(bf16)


def last_up(block, high, low, out, scale, sums):
    total = jnp.zeros((COLS, 128), f32)
    h = high[0:COLS, 0:RANK]
    for z in range(NZ):
        r = block[z].astype(f32) + jnp.dot(
            h, low[:, 640 * z : 640 * z + 640], preferred_element_type=f32
        )
        sums[:, 640 * z : 640 * z + 640] = r
        total = total + magnitudes(r)
    column, row = scales(total)
    scale[...] = row
    out[...] = (sums[...] * (1.0 / column)).astype(bf16)


def kernel(body, outs, scratch=()):
    return pl.pallas_call(
        body,
        out_shape=[jax.ShapeDtypeStruct(*o) for o in outs],
        scratch_shapes=list(scratch),
        compiler_params=pltpu.CompilerParams(vmem_limit_bytes=48 * 2**20),
    )


def along_z(x):
    flat = x.reshape(-1, x.shape[-1])
    return lax.all_to_all(
        flat, "zero", 0, 0, axis_index_groups=Z_GROUPS, tiled=True
    ).reshape(x.shape)


def across(parts):
    moved = [
        lax.ppermute(part, "zero", [(s, s ^ p) for s in range(NZ * NQ)])
        for p, part in enumerate(parts)
        if p
    ]
    return [parts[0], *moved]


def local(weight_gate, low_gate, high_gate, weight_up, low_up, high_up, norm_train, norm_step):
    (block,) = kernel(pack_gate, [((NZ, BLOCK, 128), bf16)])(
        weight_gate, low_gate.T, low_up.T, norm_train[None], norm_step[None]
    )
    block_in = along_z(block)
    *up_parts, mix, high = kernel(
        pack_up, [((NZ, 2 * ROWS, 128), bf16)] * NQ + [((256, 256), bf16), ((256, 128), bf16)]
    )(weight_up, high_gate, high_up)
    up_parts = across(up_parts)
    (up_block,) = kernel(
        turn_up, [((NZ, COLS, 640), bf16)], [pltpu.VMEM((2, NQ * ROWS, 256), bf16)]
    )(*up_parts)
    up_in = along_z(up_block)
    parts = kernel(split_gate, [((NZ, PART, 128), bf16)] * NQ)(block_in)
    parts = across(parts)
    final_gate, scale_gate, low, norm = kernel(
        last_gate,
        [((COLS, D_MODEL), bf16), ((1, COLS), f32), ((RANK, D_MODEL), bf16), ((NZ, NQ, 128), f32)],
        [
            pltpu.VMEM((2, NQ * ROWS, 256), bf16),
            pltpu.VMEM((2, NQ * ROWS, 128), bf16),
            pltpu.VMEM((COLS, D_MODEL), f32),
        ],
    )(*parts, mix)
    mine = norm.reshape(NZ * NQ, 128)[:, :80].astype(bf16)
    other = lax.ppermute(mine, "cols", [(0, 1), (1, 0)])
    first = lax.axis_index("cols") == 0
    serve_norm = jnp.stack(
        [jnp.where(first, mine, other), jnp.where(first, other, mine)], axis=1
    ).reshape(D_MODEL)
    final_up, scale_up = kernel(
        last_up, [((COLS, D_MODEL), bf16), ((1, COLS), f32)], [pltpu.VMEM((COLS, D_MODEL), f32)]
    )(up_in, high, low)
    return (final_gate.T, final_up.T, scale_gate[0], scale_up[0], serve_norm)


def solution(mesh):
    in_specs = (
        P(("unit", "zero"), "cols"),
        P(("unit", "zero"), None),
        P("unit", "cols"),
        P(("unit", "zero"), "cols"),
        P(("unit", "zero"), None),
        P("unit", "cols"),
        P(("unit", "zero", "cols")),
        P(("unit", "zero", "cols")),
    )
    out_specs = (
        P("unit", ("cols", "zero")),
        P("unit", ("cols", "zero")),
        P(("unit", "cols", "zero")),
        P(("unit", "cols", "zero")),
        P("unit"),
    )
    return jax.shard_map(local, mesh=mesh, in_specs=in_specs, out_specs=out_specs, check_vma=False)
```

time: 245 us -> 138 us (0.56); the launches traced: 241 us -> 137 us
  waiting for transfers between devices: 141 us -> 86 us
  local copies, waits for them, and re-layouts: 39.1 us -> 9.49 us
  starting transfers between devices: 44.4 us -> 27 us
  Pallas kernels: 0 us -> 13.9 us
  matrix products: 7.77 us -> 0 us
  other arithmetic: 7.35 us -> 0.02 us
    all_to_all x4 -> x2, waiting for transfers between devices: 141 us -> 25.6 us  [along_z(): lax.all_to_all(flat, 'zero', 0, 0, axis_index_groups=Z_GROUPS, tiled=True)]
    ppermute x0 -> x7, waiting for transfers between devices: none -> 60.4 us  [the longest x6 60.4 us: across(): lax.ppermute(part, 'zero', [(s, s ^ p) for s in range(NZ * NQ)])]
    all_to_all x4 -> x2, starting transfers between devices: 44.4 us -> 13 us  [along_z(): lax.all_to_all(flat, 'zero', 0, 0, axis_index_groups=Z_GROUPS, tiled=True)]
    all_to_all x4 -> x0, local copies, waits for them, and re-layouts: 26.6 us -> none  [the longest x2 14.6 us: local(): lax.all_to_all(narrow_up, 'zero', split_axis=1, concat_axis=0, tiled=True)]
    ppermute x0 -> x7, starting transfers between devices: none -> 14 us  [the longest x6 13.2 us: across(): lax.ppermute(part, 'zero', [(s, s ^ p) for s in range(NZ * NQ)])]
    pallas_call x0 -> x6, Pallas kernels: none -> 13.9 us  [the longest x1 4.31 us: local(): kernel(last_up, [((COLS, D_MODEL), bf16), ((1, COLS), f32)], [pltpu.VMEM(...]
    dot_general x2 -> x0, matrix products: 7.77 us -> none  [the longest x1 4.67 us: local(): jnp.dot(low_up, high_up, preferred_element_type=jnp.float32)]
    convert_element_type x2 -> x0, other arithmetic: 6.22 us -> none  [the longest x1 6.22 us: local(): (result_up / scale_up).astype(jnp.bfloat16)]
  transfers between devices with their start and end apart: 4 -> 9, of which waited for: 3 -> 8; matrix products, arithmetic and copies ran while one was open for 8% -> 0% of each run, Pallas kernels for 0% -> 9%
where the time goes in v1:
time: 138 us; the launch traced here: 137 us
  waiting for transfers between devices  86 us (62%)
  starting transfers between devices  27 us (20%)
  Pallas kernels  13.9 us (10%)
  local copies, waits for them, and re-layouts  9.49 us (7%)
    ppermute x6, waiting for transfers between devices, across(): lax.ppermute(part, 'zero', [(s, s ^ p) for s in range(NZ * NQ)])  60.4 us
    all_to_all x2, waiting for transfers between devices, along_z(): lax.all_to_all(flat, 'zero', 0, 0, axis_index_groups=Z_GROUPS, tiled=True)  25.6 us
    ppermute x6, starting transfers between devices, across(): lax.ppermute(part, 'zero', [(s, s ^ p) for s in range(NZ * NQ)])  13.2 us
    all_to_all x2, starting transfers between devices, along_z(): lax.all_to_all(flat, 'zero', 0, 0, axis_index_groups=Z_GROUPS, tiled=True)  13 us
    unnamed x20, local copies, waits for them, and re-layouts  8.78 us
    pallas_call x1, Pallas kernels, local(): kernel(last_up, [((COLS, D_MODEL), bf16), ((1, COLS), f32)], [pltpu.VMEM(...  4.31 us
    pallas_call x1, Pallas kernels, local(): kernel(last_gate, [((COLS, D_MODEL), bf16), ((1, COLS), f32), ((RANK, D_M...  3.67 us
  transfers between devices with their start and end apart: 9, of which 8 were waited for; matrix products, arithmetic and copies ran while one was open for 0% of the time, Pallas kernels for 9%

profile of v1, /device:TPU:6, one launch (start us, length us, event | category | flops | bytes accessed | tf_op | source)
XLA Modules:
  0.0 137.2 jit_solution(11027997624062670184)
XLA Ops:
  0.6 1.6 %copy-done.2 = bf16[160,6912]{1,0:T(8,128)(2,1)S(1)} copy-done((bf16[160,6912]{1,0:T(8,128)(2,1)S(1)}, bf16[160,6912]{1,0:T(8,128)(2,1)}, u32[]{:S(2)}) %copy-start.2) | copy-done | bytes 2211864
  2.3 0.7 copy-done.6
  3.0 0.7 copy-done.7
  3.7 0.7 copy-done.8
  4.4 0.7 copy-done.9
  5.0 1.0 shard_map.119
  6.0 1.4 %copy-done = bf16[8,1168,128]{2,1,0:T(8,128)(2,1)} copy-done((bf16[8,1168,128]{2,1,0:T(8,128)(2,1)}, bf16[8,1168,128]{2,1,0:T(8,128)(2,1)S(1)}, u32[]{:S(2)}) %copy-start) | copy-done | bytes 2392088
  7.5 8.6 %all-to-all-start = ((bf16[8,1168,128]{2,1,0:T(8,128)(2,1)}), bf16[8,1168,128]{2,1,0:T(8,128)(2,1)S(1)}, u32[]{:S(2)}, u32[]{:S(2)}) async-start(bf16[8,1168,128]{2,1,0:T(8,128)(2,1)} %copy-done), calls=%async_computation | async-start | bytes 4784128 | tf_op jit(solution)/shard_map/all_to_all | solution.py:206
  16.1 1.6 %copy-done.3 = bf16[160,6912]{1,0:T(8,128)(2,1)S(1)} copy-done((bf16[160,6912]{1,0:T(8,128)(2,1)S(1)}, bf16[160,6912]{1,0:T(8,128)(2,1)}, u32[]{:S(2)}) %copy-start.3) | copy-done | bytes 2211864
  17.7 1.8 %shard_map.121 = (bf16[8,320,128]{2,1,0:T(8,128)(2,1)S(1)}, bf16[8,320,128]{2,1,0:T(8,128)(2,1)S(1)}, bf16[8,320,128]{2,1,0:T(8,128)(2,1)S(1)}, bf16[8,320,128]{...) custom-call(bf16[160,6912]{1,0:T(8,128)(2,1)S(1)} %copy-done.3, ...), custom_call_target="tpu_custom_call" | custom-call | tf_op jit(solution)/shard_map/pallas_call | solution.py:225
  19.5 1.5 %collective-permute-start.3 = (bf16[8,320,128]{2,1,0:T(8,128)(2,1)S(1)}, bf16[8,320,128]{2,1,0:T(8,128)(2,1)S(1)}, u32[]{:S(2)}, u32[]{:S(2)}) collective-permute-start(bf16[8,320,128]{2,1,0:T(8,128)(2,1)S(1)} %get-tuple-element.28), channel_id=1, source_target_pairs={{0,2},{2,0},{4,6},{6,4},{8,10},{10,8},{12,14},{14,12},{16,18},{18,... | collective-permute-start | bytes 1966088 | tf_op jit(solution)/shard_map/ppermute | solution.py:213
  21.0 3.2 %collective-permute-start.4 = (bf16[8,320,128]{2,1,0:T(8,128)(2,1)S(1)}, bf16[8,320,128]{2,1,0:T(8,128)(2,1)S(1)}, u32[]{:S(2)}, u32[]{:S(2)}) collective-permute-start(bf16[8,320,128]{2,1,0:T(8,128)(2,1)S(1)} %get-tuple-element.29), channel_id=1, source_target_pairs={{0,4},{2,6},{4,0},{6,2},{8,12},{10,14},{12,8},{14,10},{16,20},{18,... | collective-permute-start | bytes 1966088 | tf_op jit(solution)/shard_map/ppermute | solution.py:213
  24.2 1.9 %collective-permute-start.5 = (bf16[8,320,128]{2,1,0:T(8,128)(2,1)S(1)}, bf16[8,320,128]{2,1,0:T(8,128)(2,1)S(1)}, u32[]{:S(2)}, u32[]{:S(2)}) collective-permute-start(bf16[8,320,128]{2,1,0:T(8,128)(2,1)S(1)} %get-tuple-element.30), channel_id=1, source_target_pairs={{0,6},{2,4},{4,2},{6,0},{8,14},{10,12},{12,10},{14,8},{16,22},{18,... | collective-permute-start | bytes 1966088 | tf_op jit(solution)/shard_map/ppermute | solution.py:213
  26.1 12.6 %collective-permute-done.3.refs_1_ = bf16[8,320,128]{2,1,0:T(8,128)(2,1)S(1)} collective-permute-done((bf16[8,320,128]{2,1,0:T(8,128)(2,1)S(1)}, bf16[8,320,128]{2,1,0:T(8,128)(2,1)S(1)}, u32[]{:S(2)}, u32[]{:S(2)}) %collective-permute-start.3) | collective-permute-done | bytes 655392 | tf_op jit(solution)/shard_map/ppermute | solution.py:213
  38.7 13.0 %collective-permute-done.4.refs_2_ = bf16[8,320,128]{2,1,0:T(8,128)(2,1)S(1)} collective-permute-done((bf16[8,320,128]{2,1,0:T(8,128)(2,1)S(1)}, bf16[8,320,128]{2,1,0:T(8,128)(2,1)S(1)}, u32[]{:S(2)}, u32[]{:S(2)}) %collective-permute-start.4) | collective-permute-done | bytes 655392 | tf_op jit(solution)/shard_map/ppermute | solution.py:213
  51.7 2.3 %collective-permute-done.5.refs_3_ = bf16[8,320,128]{2,1,0:T(8,128)(2,1)S(1)} collective-permute-done((bf16[8,320,128]{2,1,0:T(8,128)(2,1)S(1)}, bf16[8,320,128]{2,1,0:T(8,128)(2,1)S(1)}, u32[]{:S(2)}, u32[]{:S(2)}) %collective-permute-start.5) | collective-permute-done | bytes 655392 | tf_op jit(solution)/shard_map/ppermute | solution.py:213
  54.0 1.2 shard_map.123
  55.2 1.3 copy-done.1
  56.6 17.0 %all-to-all-done.block = bf16[8,1168,128]{2,1,0:T(8,128)(2,1)S(1)} async-done(((bf16[8,1168,128]{2,1,0:T(8,128)(2,1)}), bf16[8,1168,128]{2,1,0:T(8,128)(2,1)S(1)}, u32[]{:S(2)}, u32[]{:S(2)}) %all-to-all-start) | async-done | bytes 2392096 | tf_op jit(solution)/shard_map/all_to_all | solution.py:206
  73.6 4.4 %all-to-all-start.1 = ((bf16[8,216,640]{2,1,0:T(8,128)(2,1)}), bf16[8,216,640]{2,1,0:T(8,128)(2,1)}, u32[]{:S(2)}, u32[]{:S(2)}) async-start(bf16[8,216,640]{2,1,0:T(8,128)(2,1)} %copy-done.1), calls=%async_computation.1 | async-start | bytes 4423680 | tf_op jit(solution)/shard_map/all_to_all | solution.py:206
  78.0 1.9 %shard_map.120 = (bf16[8,368,128]{2,1,0:T(8,128)(2,1)S(1)}, bf16[8,368,128]{2,1,0:T(8,128)(2,1)S(1)}, bf16[8,368,128]{2,1,0:T(8,128)(2,1)S(1)}, bf16[8,368,128]{2,1,0:T(8,128)(2,1)S(1)}) custom-call(bf16[8,1168,128]{2,1,0:T(8,128)(2,1)S(1)} %all-to-all-done.block), custom_call_target="tpu_custom_call" | custom-call | tf_op jit(solution)/shard_map/pallas_call | solution.py:233
  79.9 1.5 %collective-permute-start = (bf16[8,368,128]{2,1,0:T(8,128)(2,1)S(1)}, bf16[8,368,128]{2,1,0:T(8,128)(2,1)S(1)}, u32[]{:S(2)}, u32[]{:S(2)}) collective-permute-start(bf16[8,368,128]{2,1,0:T(8,128)(2,1)S(1)} %get-tuple-element.22), channel_id=1, source_target_pairs={{0,2},{2,0},{4,6},{6,4},{8,10},{10,8},{12,14},{14,12},{16,18},{18,... | collective-permute-start | bytes 2261000 | tf_op jit(solution)/shard_map/ppermute | solution.py:213
  81.4 3.2 %collective-permute-start.1 = (bf16[8,368,128]{2,1,0:T(8,128)(2,1)S(1)}, bf16[8,368,128]{2,1,0:T(8,128)(2,1)S(1)}, u32[]{:S(2)}, u32[]{:S(2)}) collective-permute-start(bf16[8,368,128]{2,1,0:T(8,128)(2,1)S(1)} %get-tuple-element.23), channel_id=1, source_target_pairs={{0,4},{2,6},{4,0},{6,2},{8,12},{10,14},{12,8},{14,10},{16,20},{18,... | collective-permute-start | bytes 2261000 | tf_op jit(solution)/shard_map/ppermute | solution.py:213
  84.6 1.9 %collective-permute-start.2 = (bf16[8,368,128]{2,1,0:T(8,128)(2,1)S(1)}, bf16[8,368,128]{2,1,0:T(8,128)(2,1)S(1)}, u32[]{:S(2)}, u32[]{:S(2)}) collective-permute-start(bf16[8,368,128]{2,1,0:T(8,128)(2,1)S(1)} %get-tuple-element.24), channel_id=1, source_target_pairs={{0,6},{2,4},{4,2},{6,0},{8,14},{10,12},{12,10},{14,8},{16,22},{18,... | collective-permute-start | bytes 2261000 | tf_op jit(solution)/shard_map/ppermute | solution.py:213
  86.5 14.7 %collective-permute-done.refs_1_ = bf16[8,368,128]{2,1,0:T(8,128)(2,1)S(1)} collective-permute-done((bf16[8,368,128]{2,1,0:T(8,128)(2,1)S(1)}, bf16[8,368,128]{2,1,0:T(8,128)(2,1)S(1)}, u32[]{:S(2)}, u32[]{:S(2)}) %collective-permute-start) | collective-permute-done | bytes 753696 | tf_op jit(solution)/shard_map/ppermute | solution.py:213
  101.2 15.5 %collective-permute-done.1.refs_2_ = bf16[8,368,128]{2,1,0:T(8,128)(2,1)S(1)} collective-permute-done((bf16[8,368,128]{2,1,0:T(8,128)(2,1)S(1)}, bf16[8,368,128]{2,1,0:T(8,128)(2,1)S(1)}, u32[]{:S(2)}, u32[]{:S(2)}) %collective-permute-start.1) | collective-permute-done | bytes 753696 | tf_op jit(solution)/shard_map/ppermute | solution.py:213
  116.7 2.3 %collective-permute-done.2.refs_3_ = bf16[8,368,128]{2,1,0:T(8,128)(2,1)S(1)} collective-permute-done((bf16[8,368,128]{2,1,0:T(8,128)(2,1)S(1)}, bf16[8,368,128]{2,1,0:T(8,128)(2,1)S(1)}, u32[]{:S(2)}, u32[]{:S(2)}) %collective-permute-start.2) | collective-permute-done | bytes 753696 | tf_op jit(solution)/shard_map/ppermute | solution.py:213
  119.0 3.7 %shard_map.122 = (bf16[216,5120]{1,0:T(8,128)(2,1)}, f32[1,216]{1,0:T(1,128)}, bf16[32,5120]{1,0:T(8,128)(2,1)S(1)}, f32[8,4,128]{2,1,0:T(4,128)S(1)}) custom-call(bf16[8,368,128]{2,1,0:T(8,128)(2,1)S(1)} %get-tuple-element.21.refs_0_, bf16[8,368,128]{2,1,0:T(8,128)(2,1)S(1)} %collective-permute-done.refs_1_, ...), custom_call_target="tpu_custom_call" | custom-call | tf_op jit(solution)/shard_map/pallas_call | solution.py:235
  122.7 0.8 collective-permute-start.6
  123.5 8.6 %all-to-all-done.1.block = bf16[8,216,640]{2,1,0:T(8,128)(2,1)} async-done(((bf16[8,216,640]{2,1,0:T(8,128)(2,1)}), bf16[8,216,640]{2,1,0:T(8,128)(2,1)}, u32[]{:S(2)}, u32[]{:S(2)}) %all-to-all-start.1) | async-done | bytes 2211872 | tf_op jit(solution)/shard_map/all_to_all | solution.py:206
  132.1 4.3 %shard_map.124 = (bf16[216,5120]{1,0:T(8,128)(2,1)}, f32[1,216]{1,0:T(1,128)}) custom-call(bf16[8,216,640]{2,1,0:T(8,128)(2,1)} %all-to-all-done.1.block, bf16[256,128]{1,0:T(8,128)(2,1)S(1)} %get-tuple-element.31.high, bf16[32,5120]{1,0:T(8,128)(2,1)S(1)} %get-tuple-element.32.low), custom_call_target="tpu_custom_call" | custom-call | tf_op jit(solution)/shard_map/pallas_call | solution.py:250
  136.5 0.7 reshape.30
  (17 shorter events, 0.1 us)
Async XLA Ops:
  0.6 1.6 %copy-start.2 = (bf16[160,6912]{1,0:T(8,128)(2,1)S(1)}, bf16[160,6912]{1,0:T(8,128)(2,1)}, u32[]{:S(2)}) copy-start(bf16[160,6912]{1,0:T(8,128)(2,1)} %weight.2) | copy-start | bytes 6635524
  2.3 0.7 copy-start.6
  3.0 0.7 copy-start.7
  3.7 0.7 copy-start.8
  4.3 0.7 copy-start.9
  6.0 1.4 %copy-start = (bf16[8,1168,128]{2,1,0:T(8,128)(2,1)}, bf16[8,1168,128]{2,1,0:T(8,128)(2,1)S(1)}, u32[]{:S(2)}) copy-start(bf16[8,1168,128]{2,1,0:T(8,128)(2,1)S(1)} %shard_map.119) | copy-start | bytes 7176196
  7.5 8.6 %copy-start.4 = (bf16[32,6912]{1,0:T(8,128)(2,1)S(1)}, bf16[32,6912]{1,0:T(8,128)(2,1)}, u32[]{:S(2)}) copy-start(bf16[32,6912]{1,0:T(8,128)(2,1)} %high_gate.1) | copy-start | bytes 1327108
  7.5 8.6 %copy-start.5 = (bf16[32,6912]{1,0:T(8,128)(2,1)S(1)}, bf16[32,6912]{1,0:T(8,128)(2,1)}, u32[]{:S(2)}) copy-start(bf16[32,6912]{1,0:T(8,128)(2,1)} %high_up.1) | copy-start | bytes 1327108
  7.5 66.1 %all-to-all-start = ((bf16[8,1168,128]{2,1,0:T(8,128)(2,1)}), bf16[8,1168,128]{2,1,0:T(8,128)(2,1)S(1)}, u32[]{:S(2)}, u32[]{:S(2)}) async-start(bf16[8,1168,128]{2,1,0:T(8,128)(2,1)} %copy-done), calls=%async_computation | async-start | bytes 4784128 | tf_op jit(solution)/shard_map/all_to_all | solution.py:206
  16.1 1.6 %copy-start.3 = (bf16[160,6912]{1,0:T(8,128)(2,1)S(1)}, bf16[160,6912]{1,0:T(8,128)(2,1)}, u32[]{:S(2)}) copy-start(bf16[160,6912]{1,0:T(8,128)(2,1)} %weight.3) | copy-start | bytes 6635524
  19.5 19.2 %collective-permute-start.3 = (bf16[8,320,128]{2,1,0:T(8,128)(2,1)S(1)}, bf16[8,320,128]{2,1,0:T(8,128)(2,1)S(1)}, u32[]{:S(2)}, u32[]{:S(2)}) collective-permute-start(bf16[8,320,128]{2,1,0:T(8,128)(2,1)S(1)} %get-tuple-element.28), channel_id=1, source_target_pairs={{0,2},{2,0},{4,6},{6,4},{8,10},{10,8},{12,14},{14,12},{16,18},{18,... | collective-permute-start | bytes 1966088 | tf_op jit(solution)/shard_map/ppermute | solution.py:213
  21.0 30.7 %collective-permute-start.4 = (bf16[8,320,128]{2,1,0:T(8,128)(2,1)S(1)}, bf16[8,320,128]{2,1,0:T(8,128)(2,1)S(1)}, u32[]{:S(2)}, u32[]{:S(2)}) collective-permute-start(bf16[8,320,128]{2,1,0:T(8,128)(2,1)S(1)} %get-tuple-element.29), channel_id=1, source_target_pairs={{0,4},{2,6},{4,0},{6,2},{8,12},{10,14},{12,8},{14,10},{16,20},{18,... | collective-permute-start | bytes 1966088 | tf_op jit(solution)/shard_map/ppermute | solution.py:213
  24.2 29.8 %collective-permute-start.5 = (bf16[8,320,128]{2,1,0:T(8,128)(2,1)S(1)}, bf16[8,320,128]{2,1,0:T(8,128)(2,1)S(1)}, u32[]{:S(2)}, u32[]{:S(2)}) collective-permute-start(bf16[8,320,128]{2,1,0:T(8,128)(2,1)S(1)} %get-tuple-element.30), channel_id=1, source_target_pairs={{0,6},{2,4},{4,2},{6,0},{8,14},{10,12},{12,10},{14,8},{16,22},{18,... | collective-permute-start | bytes 1966088 | tf_op jit(solution)/shard_map/ppermute | solution.py:213
  55.2 1.4 copy-start.1
  73.6 58.5 %all-to-all-start.1 = ((bf16[8,216,640]{2,1,0:T(8,128)(2,1)}), bf16[8,216,640]{2,1,0:T(8,128)(2,1)}, u32[]{:S(2)}, u32[]{:S(2)}) async-start(bf16[8,216,640]{2,1,0:T(8,128)(2,1)} %copy-done.1), calls=%async_computation.1 | async-start | bytes 4423680 | tf_op jit(solution)/shard_map/all_to_all | solution.py:206
  79.9 21.3 %collective-permute-start = (bf16[8,368,128]{2,1,0:T(8,128)(2,1)S(1)}, bf16[8,368,128]{2,1,0:T(8,128)(2,1)S(1)}, u32[]{:S(2)}, u32[]{:S(2)}) collective-permute-start(bf16[8,368,128]{2,1,0:T(8,128)(2,1)S(1)} %get-tuple-element.22), channel_id=1, source_target_pairs={{0,2},{2,0},{4,6},{6,4},{8,10},{10,8},{12,14},{14,12},{16,18},{18,... | collective-permute-start | bytes 2261000 | tf_op jit(solution)/shard_map/ppermute | solution.py:213
  81.4 35.3 %collective-permute-start.1 = (bf16[8,368,128]{2,1,0:T(8,128)(2,1)S(1)}, bf16[8,368,128]{2,1,0:T(8,128)(2,1)S(1)}, u32[]{:S(2)}, u32[]{:S(2)}) collective-permute-start(bf16[8,368,128]{2,1,0:T(8,128)(2,1)S(1)} %get-tuple-element.23), channel_id=1, source_target_pairs={{0,4},{2,6},{4,0},{6,2},{8,12},{10,14},{12,8},{14,10},{16,20},{18,... | collective-permute-start | bytes 2261000 | tf_op jit(solution)/shard_map/ppermute | solution.py:213
  84.6 34.4 %collective-permute-start.2 = (bf16[8,368,128]{2,1,0:T(8,128)(2,1)S(1)}, bf16[8,368,128]{2,1,0:T(8,128)(2,1)S(1)}, u32[]{:S(2)}, u32[]{:S(2)}) collective-permute-start(bf16[8,368,128]{2,1,0:T(8,128)(2,1)S(1)} %get-tuple-element.24), channel_id=1, source_target_pairs={{0,6},{2,4},{4,2},{6,0},{8,14},{10,12},{12,10},{14,8},{16,22},{18,... | collective-permute-start | bytes 2261000 | tf_op jit(solution)/shard_map/ppermute | solution.py:213
  122.7 13.7 %collective-permute-start.6 = (bf16[32,80]{1,0:T(8,128)(2,1)S(1)}, bf16[32,80]{1,0:T(8,128)(2,1)S(1)}, u32[]{:S(2)}, u32[]{:S(2)}) collective-permute-start(bf16[32,80]{1,0:T(8,128)(2,1)S(1)} %bitcast.18), channel_id=1, source_target_pairs={{0,1},{1,0},{2,3},{3,2},{4,5},{5,4},{6,7},{7,6},{8,9},{9,8},{10,11... | collective-permute-start | bytes 15368 | tf_op jit(solution)/shard_map/ppermute | solution.py:245

commit v2 on v1

--- a/solution.py
+++ b/solution.py
@@ -4,6 +4,7 @@
 from jax.experimental import pallas as pl
 from jax.experimental.pallas import tpu as pltpu
 from jax.sharding import PartitionSpec as P
+
 
 D_MODEL = 5120
 MIX = 0.5
@@ -19,7 +20,7 @@
 PART = 2 * ROWS + EXTRA
 LAST = 51
 
-Z_GROUPS = [[z * NQ + q for z in range(NZ)] for q in range(NQ)]
+SHIFTS = (4, 3, 5, 2, 6, 1, 7)
 bf16, f32 = jnp.bfloat16, jnp.float32
 
 
@@ -39,7 +40,7 @@
     )
 
 
-def pack_gate(weight, low_gate, low_up, train, step, out):
+def pack_gate(weight, low_gate, low_up, train, step, *outs):
     wide = (ROWS, 128)
     low_g = place_t(low_gate[...], 128, 96)
     low_u = place_t(low_up[...], 32, 0)
@@ -50,20 +51,18 @@
     norm = jnp.concatenate([train[...] + step[...], jnp.zeros((1, 48), f32)], axis=1)
     norm = jnp.broadcast_to(norm, (8, 128))
     extra = jnp.concatenate([packed, norm], axis=0).astype(bf16)
-    for z in range(NZ):
-        first, off = divmod(SPAN * z, 128)
+    here = lax.axis_index("zero") // NQ
+    for k in range(NZ):
+        start = SPAN * ((here + k) % NZ)
+        tile = jnp.minimum(start // 128, LAST - 5)
+        x = weight[:, pl.ds(pl.multiple_of(tile * 128, 128), 1024)].astype(f32)
+        x = pltpu.roll(x, (1024 - (start - 128 * tile)) % 1024, 1)
         for j in range(TILES):
-            t = first + j
-            x = weight[:, 128 * t : 128 * t + 128].astype(f32)
-            if off:
-                x = pltpu.roll(x, 128 - off, 1)
-                if j < TILES - 1 or off > 32:
-                    y = weight[:, 128 * t + 128 : 128 * t + 256].astype(f32)
-                    x = jnp.where(lanes(wide) < 128 - off, x, pltpu.roll(y, 128 - off, 1))
+            y = x[:, 128 * j : 128 * j + 128]
             if j == TILES - 1:
-                x = jnp.where(lanes(wide) < 96, x, low_g)
-            out[z, ROWS * j : ROWS * j + ROWS, :] = x.astype(bf16)
-        out[z, ROWS * TILES : BLOCK, :] = extra
+                y = jnp.where(lanes(wide) < 96, y, low_g)
+            outs[k][ROWS * j : ROWS * j + ROWS, :] = y.astype(bf16)
+        outs[k][ROWS * TILES : BLOCK, :] = extra
 
 
 def window(x, off):
@@ -101,31 +100,36 @@
 
 
 def turn_up(*refs):
-    parts, out, x = refs[:NQ], refs[NQ], refs[NQ + 1]
-    q = lax.axis_index("zero") % NQ
+    parts, outs, x = refs[:NQ], refs[NQ : NQ + NZ], refs[NQ + NZ]
+    place = lax.axis_index("zero")
+    q, here = place % NQ, place // NQ
     eye = (lanes((COLS, 256)) == rows((COLS, 256))).astype(bf16)
-    for z in range(NZ):
+    for k in range(NZ):
+        z = (here + k) % NZ
         for p in range(NQ):
             at = pl.multiple_of(jnp.bitwise_xor(q, p) * ROWS, ROWS)
-            x[z % 2, pl.ds(at, ROWS), 0:128] = parts[p][z, 0:ROWS, :]
-            x[z % 2, pl.ds(at, ROWS), 128:256] = parts[p][z, ROWS : 2 * ROWS, :]
-        out[z] = lax.dot_general(
-            eye, x[z % 2], (((1,), (1,)), ((), ())), preferred_element_type=f32
+            x[k % 2, pl.ds(at, ROWS), 0:128] = parts[p][z, 0:ROWS, :]
+            x[k % 2, pl.ds(at, ROWS), 128:256] = parts[p][z, ROWS : 2 * ROWS, :]
+        outs[k][...] = lax.dot_general(
+            eye, x[k % 2], (((1,), (1,)), ((), ())), preferred_element_type=f32
         ).astype(bf16)
 
 
-def split_gate(block, *parts):
-    q = lax.axis_index("zero") % NQ
+def split_gate(*refs):
+    blocks, parts = refs[:NZ], refs[NZ:]
+    place = lax.axis_index("zero")
+    q, here = place % NQ, place // NQ
     wide = (ROWS, 128)
-    for z in range(NZ):
-        low = pltpu.roll(block[z, ROWS * 6 : ROWS * 7, :].astype(f32), 120, 1)
+    for k, block in enumerate(blocks):
+        z = (here + NZ - k) % NZ
+        low = pltpu.roll(block[ROWS * 6 : ROWS * 7, :].astype(f32), 120, 1)
         for p in range(NQ):
             start = COLS * jnp.bitwise_xor(q, p)
             tile = jnp.minimum(start // 128, TILES - 3)
             x = jnp.concatenate(
                 [
-                    block[z, pl.ds(pl.multiple_of((tile + k) * ROWS, ROWS), ROWS), :].astype(f32)
-                    for k in range(3)
+                    block[pl.ds(pl.multiple_of((tile + n) * ROWS, ROWS), ROWS), :].astype(f32)
+                    for n in range(3)
                 ],
                 axis=1,
             )
@@ -133,7 +137,7 @@
             last = jnp.where(lanes(wide) < 88, x[:, 128:], jnp.where(lanes(wide) < 120, low, 0.0))
             parts[p][z, 0:ROWS, :] = x[:, :128].astype(bf16)
             parts[p][z, ROWS : 2 * ROWS, :] = last.astype(bf16)
-            parts[p][z, 2 * ROWS : PART, :] = block[z, ROWS * TILES : BLOCK, :]
+            parts[p][z, 2 * ROWS : PART, :] = block[ROWS * TILES : BLOCK, :]
 
 
 def scales(total):
@@ -178,14 +182,18 @@
     out[...] = (sums[...] * (1.0 / column)).astype(bf16)
 
 
-def last_up(block, high, low, out, scale, sums):
+def last_up(*refs):
+    blocks, high, low = refs[:NZ], refs[NZ], refs[NZ + 1]
+    out, scale, sums = refs[NZ + 2 :]
+    here = lax.axis_index("zero") // NQ
     total = jnp.zeros((COLS, 128), f32)
     h = high[0:COLS, 0:RANK]
-    for z in range(NZ):
-        r = block[z].astype(f32) + jnp.dot(
-            h, low[:, 640 * z : 640 * z + 640], preferred_element_type=f32
+    for k in range(NZ):
+        at = pl.multiple_of((here + NZ - k) % NZ * 640, 640)
+        r = blocks[k][...].astype(f32) + jnp.dot(
+            h, low[:, pl.ds(at, 640)], preferred_element_type=f32
         )
-        sums[:, 640 * z : 640 * z + 640] = r
+        sums[:, pl.ds(at, 640)] = r
         total = total + magnitudes(r)
     column, row = scales(total)
     scale[...] = row
@@ -201,11 +209,12 @@
     )
 
 
-def along_z(x):
-    flat = x.reshape(-1, x.shape[-1])
-    return lax.all_to_all(
-        flat, "zero", 0, 0, axis_index_groups=Z_GROUPS, tiled=True
-    ).reshape(x.shape)
+def along_z(blocks):
+    moved = list(blocks)
+    for k in SHIFTS:
+        pairs = [(z * NQ + q, (z + k) % NZ * NQ + q) for z in range(NZ) for q in range(NQ)]
+        moved[k] = lax.ppermute(blocks[k], "zero", pairs)
+    return moved
 
 
 def across(parts):
@@ -218,19 +227,19 @@
 
 
 def local(weight_gate, low_gate, high_gate, weight_up, low_up, high_up, norm_train, norm_step):
-    (block,) = kernel(pack_gate, [((NZ, BLOCK, 128), bf16)])(
+    blocks = kernel(pack_gate, [((BLOCK, 128), bf16)] * NZ)(
         weight_gate, low_gate.T, low_up.T, norm_train[None], norm_step[None]
     )
-    block_in = along_z(block)
+    blocks_in = along_z(blocks)
     *up_parts, mix, high = kernel(
         pack_up, [((NZ, 2 * ROWS, 128), bf16)] * NQ + [((256, 256), bf16), ((256, 128), bf16)]
     )(weight_up, high_gate, high_up)
     up_parts = across(up_parts)
-    (up_block,) = kernel(
-        turn_up, [((NZ, COLS, 640), bf16)], [pltpu.VMEM((2, NQ * ROWS, 256), bf16)]
+    up_blocks = kernel(
+        turn_up, [((COLS, 640), bf16)] * NZ, [pltpu.VMEM((2, NQ * ROWS, 256), bf16)]
     )(*up_parts)
-    up_in = along_z(up_block)
-    parts = kernel(split_gate, [((NZ, PART, 128), bf16)] * NQ)(block_in)
+    up_in = along_z(up_blocks)
+    parts = kernel(split_gate, [((NZ, PART, 128), bf16)] * NQ)(*blocks_in)
     parts = across(parts)
     final_gate, scale_gate, low, norm = kernel(
         last_gate,
@@ -249,7 +258,7 @@
     ).reshape(D_MODEL)
     final_up, scale_up = kernel(
         last_up, [((COLS, D_MODEL), bf16), ((1, COLS), f32)], [pltpu.VMEM((COLS, D_MODEL), f32)]
-    )(up_in, high, low)
+    )(*up_in, high, low)
     return (final_gate.T, final_up.T, scale_gate[0], scale_up[0], serve_norm)
 
 

time: 138 us -> 178 us (1.29)
  the two profiles are of different devices: /device:TPU:6 before, /device:TPU:34 now
where the time goes in v2:
time: 178 us
  waiting for transfers between devices  100 us (56%)
  starting transfers between devices  56.8 us (32%)
  Pallas kernels  13.3 us (7%)
  local copies, waits for them, and re-layouts  7.1 us (4%)
    ppermute x14, waiting for transfers between devices, along_z(): moved[k] = lax.ppermute(blocks[k], 'zero', pairs)  100 us
    ppermute x14, starting transfers between devices, along_z(): moved[k] = lax.ppermute(blocks[k], 'zero', pairs)  39.1 us
    ppermute x6, starting transfers between devices, across(): lax.ppermute(part, 'zero', [(s, s ^ p) for s in range(NZ * NQ)])  17.6 us
    unnamed x16, local copies, waits for them, and re-layouts  6.39 us
    pallas_call x1, Pallas kernels, local(): kernel(last_gate, [((COLS, D_MODEL), bf16), ((1, COLS), f32), ((RANK, D_M...  3.69 us
  transfers between devices with their start and end apart: 21, of which 9 were waited for; matrix products, arithmetic and copies ran while one was open for 0% of the time, Pallas kernels for 7%

profile of v2, /device:TPU:34, one launch (start us, length us, event | category | flops | bytes accessed | tf_op | source)
XLA Modules:
  0.0 178.1 jit_solution(382808902547545912)
XLA Ops:
  0.6 1.6 copy-done
  5.0 1.5 shard_map.119
  6.5 2.0 %collective-permute-start = (bf16[1168,128]{1,0:T(8,128)(2,1)S(1)}, bf16[1168,128]{1,0:T(8,128)(2,1)S(1)}, u32[]{:S(2)}, u32[]{:S(2)}) collective-permute-start(bf16[1168,128]{1,0:T(8,128)(2,1)S(1)} %get-tuple-element.38), channel_id=1, source_target_pairs={{0,8},{2,10},{4,12},{6,14},{8,16},{10,18},{12,20},{14,22},{16,24},... | collective-permute-start | bytes 897032 | tf_op jit(solution)/shard_map/ppermute | solution.py:216
  8.5 1.0 copy-done.2
  10.5 1.8 %shard_map.121 = (bf16[8,320,128]{2,1,0:T(8,128)(2,1)S(1)}, bf16[8,320,128]{2,1,0:T(8,128)(2,1)S(1)}, bf16[8,320,128]{2,1,0:T(8,128)(2,1)S(1)}, bf16[8,320,128]{...) custom-call(bf16[160,6912]{1,0:T(8,128)(2,1)S(1)} %copy-done.1, ...), custom_call_target="tpu_custom_call" | custom-call | tf_op jit(solution)/shard_map/pallas_call | solution.py:234
  12.3 2.2 %collective-permute-start.10 = (bf16[8,320,128]{2,1,0:T(8,128)(2,1)S(1)}, bf16[8,320,128]{2,1,0:T(8,128)(2,1)S(1)}, u32[]{:S(2)}, u32[]{:S(2)}) collective-permute-start(bf16[8,320,128]{2,1,0:T(8,128)(2,1)S(1)} %get-tuple-element.52), channel_id=1, source_target_pairs={{0,2},{2,0},{4,6},{6,4},{8,10},{10,8},{12,14},{14,12},{16,18},{18,... | collective-permute-start | bytes 1966088 | tf_op jit(solution)/shard_map/ppermute | solution.py:222
  14.6 4.5 %collective-permute-start.1 = (bf16[1168,128]{1,0:T(8,128)(2,1)S(1)}, bf16[1168,128]{1,0:T(8,128)(2,1)S(1)}, u32[]{:S(2)}, u32[]{:S(2)}) collective-permute-start(bf16[1168,128]{1,0:T(8,128)(2,1)S(1)} %get-tuple-element.39), channel_id=1, source_target_pairs={{0,16},{2,18},{4,20},{6,22},{8,24},{10,26},{12,28},{14,30},{16,32}... | collective-permute-start | bytes 897032 | tf_op jit(solution)/shard_map/ppermute | solution.py:216
  19.0 1.9 %collective-permute-start.2 = (bf16[1168,128]{1,0:T(8,128)(2,1)S(1)}, bf16[1168,128]{1,0:T(8,128)(2,1)S(1)}, u32[]{:S(2)}, u32[]{:S(2)}) collective-permute-start(bf16[1168,128]{1,0:T(8,128)(2,1)S(1)} %get-tuple-element.40), channel_id=1, source_target_pairs={{0,24},{2,26},{4,28},{6,30},{8,32},{10,34},{12,36},{14,38},{16,40}... | collective-permute-start | bytes 897032 | tf_op jit(solution)/shard_map/ppermute | solution.py:216
  21.0 1.4 collective-permute-start.3
  22.4 3.1 %collective-permute-start.4 = (bf16[1168,128]{1,0:T(8,128)(2,1)S(1)}, bf16[1168,128]{1,0:T(8,128)(2,1)S(1)}, u32[]{:S(2)}, u32[]{:S(2)}) collective-permute-start(bf16[1168,128]{1,0:T(8,128)(2,1)S(1)} %get-tuple-element.42), channel_id=1, source_target_pairs={{0,40},{2,42},{4,44},{6,46},{8,48},{10,50},{12,52},{14,54},{16,56}... | collective-permute-start | bytes 897032 | tf_op jit(solution)/shard_map/ppermute | solution.py:216
  25.5 11.0 %collective-permute-done.1.refs_2_ = bf16[1168,128]{1,0:T(8,128)(2,1)S(1)} collective-permute-done((bf16[1168,128]{1,0:T(8,128)(2,1)S(1)}, bf16[1168,128]{1,0:T(8,128)(2,1)S(1)}, u32[]{:S(2)}, u32[]{:S(2)}) %collective-permute-start.1) | collective-permute-done | bytes 299040 | tf_op jit(solution)/shard_map/ppermute | solution.py:216
  36.7 19.9 %collective-permute-done.2.refs_3_ = bf16[1168,128]{1,0:T(8,128)(2,1)S(1)} collective-permute-done((bf16[1168,128]{1,0:T(8,128)(2,1)S(1)}, bf16[1168,128]{1,0:T(8,128)(2,1)S(1)}, u32[]{:S(2)}, u32[]{:S(2)}) %collective-permute-start.2) | collective-permute-done | bytes 299040 | tf_op jit(solution)/shard_map/ppermute | solution.py:216
  56.6 3.2 %collective-permute-start.11 = (bf16[8,320,128]{2,1,0:T(8,128)(2,1)S(1)}, bf16[8,320,128]{2,1,0:T(8,128)(2,1)S(1)}, u32[]{:S(2)}, u32[]{:S(2)}) collective-permute-start(bf16[8,320,128]{2,1,0:T(8,128)(2,1)S(1)} %get-tuple-element.53), channel_id=1, source_target_pairs={{0,4},{2,6},{4,0},{6,2},{8,12},{10,14},{12,8},{14,10},{16,20},{18,... | collective-permute-start | bytes 1966088 | tf_op jit(solution)/shard_map/ppermute | solution.py:222
  59.8 5.6 %collective-permute-start.12 = (bf16[8,320,128]{2,1,0:T(8,128)(2,1)S(1)}, bf16[8,320,128]{2,1,0:T(8,128)(2,1)S(1)}, u32[]{:S(2)}, u32[]{:S(2)}) collective-permute-start(bf16[8,320,128]{2,1,0:T(8,128)(2,1)S(1)} %get-tuple-element.54), channel_id=1, source_target_pairs={{0,6},{2,4},{4,2},{6,0},{8,14},{10,12},{12,10},{14,8},{16,22},{18,... | collective-permute-start | bytes 1966088 | tf_op jit(solution)/shard_map/ppermute | solution.py:222
  65.4 6.7 %collective-permute-done.5.refs_6_ = bf16[1168,128]{1,0:T(8,128)(2,1)S(1)} collective-permute-done((bf16[1168,128]{1,0:T(8,128)(2,1)S(1)}, bf16[1168,128]{1,0:T(8,128)(2,1)S(1)}, u32[]{:S(2)}, u32[]{:S(2)}) %collective-permute-start.5) | collective-permute-done | bytes 299040 | tf_op jit(solution)/shard_map/ppermute | solution.py:216
  72.1 4.5 %collective-permute-done.6.refs_7_ = bf16[1168,128]{1,0:T(8,128)(2,1)S(1)} collective-permute-done((bf16[1168,128]{1,0:T(8,128)(2,1)S(1)}, bf16[1168,128]{1,0:T(8,128)(2,1)S(1)}, u32[]{:S(2)}, u32[]{:S(2)}) %collective-permute-start.6) | collective-permute-done | bytes 299040 | tf_op jit(solution)/shard_map/ppermute | solution.py:216
  76.6 1.9 %shard_map.120 = (bf16[8,368,128]{2,1,0:T(8,128)(2,1)S(1)}, bf16[8,368,128]{2,1,0:T(8,128)(2,1)S(1)}, bf16[8,368,128]{2,1,0:T(8,128)(2,1)S(1)}, bf16[8,368,128]{2,1,0:T(8,128)(2,1)S(1)}) custom-call(bf16[1168,128]{1,0:T(8,128)(2,1)S(1)} %get-tuple-element.37.refs_0_, bf16[1168,128]{1,0:T(8,128)(2,1)S(1)} %collective-permute-done.refs_1_, ...), custom_call_target="tpu_custom_call" | custom-call | tf_op jit(solution)/shard_map/pallas_call | solution.py:242
  78.5 1.5 collective-permute-start.7
  80.0 3.2 %collective-permute-start.8 = (bf16[8,368,128]{2,1,0:T(8,128)(2,1)S(1)}, bf16[8,368,128]{2,1,0:T(8,128)(2,1)S(1)}, u32[]{:S(2)}, u32[]{:S(2)}) collective-permute-start(bf16[8,368,128]{2,1,0:T(8,128)(2,1)S(1)} %get-tuple-element.47), channel_id=1, source_target_pairs={{0,4},{2,6},{4,0},{6,2},{8,12},{10,14},{12,8},{14,10},{16,20},{18,... | collective-permute-start | bytes 2261000 | tf_op jit(solution)/shard_map/ppermute | solution.py:222
  83.2 1.9 %collective-permute-start.9 = (bf16[8,368,128]{2,1,0:T(8,128)(2,1)S(1)}, bf16[8,368,128]{2,1,0:T(8,128)(2,1)S(1)}, u32[]{:S(2)}, u32[]{:S(2)}) collective-permute-start(bf16[8,368,128]{2,1,0:T(8,128)(2,1)S(1)} %get-tuple-element.48), channel_id=1, source_target_pairs={{0,6},{2,4},{4,2},{6,0},{8,14},{10,12},{12,10},{14,8},{16,22},{18,... | collective-permute-start | bytes 2261000 | tf_op jit(solution)/shard_map/ppermute | solution.py:222
  85.1 1.6 shard_map.123
  86.7 14.7 %collective-permute-start.13 = (bf16[216,640]{1,0:T(8,128)(2,1)S(1)}, bf16[216,640]{1,0:T(8,128)(2,1)S(1)}, u32[]{:S(2)}, u32[]{:S(2)}) collective-permute-start(bf16[216,640]{1,0:T(8,128)(2,1)S(1)} %get-tuple-element.56), channel_id=1, source_target_pairs={{0,8},{2,10},{4,12},{6,14},{8,16},{10,18},{12,20},{14,22},{16,24},... | collective-permute-start | bytes 829448 | tf_op jit(solution)/shard_map/ppermute | solution.py:216
  101.4 12.2 %collective-permute-done.13.refs_1_ = bf16[216,640]{1,0:T(8,128)(2,1)S(1)} collective-permute-done((bf16[216,640]{1,0:T(8,128)(2,1)S(1)}, bf16[216,640]{1,0:T(8,128)(2,1)S(1)}, u32[]{:S(2)}, u32[]{:S(2)}) %collective-permute-start.13) | collective-permute-done | bytes 276512 | tf_op jit(solution)/shard_map/ppermute | solution.py:216
  113.6 27.7 %collective-permute-done.14.refs_2_ = bf16[216,640]{1,0:T(8,128)(2,1)S(1)} collective-permute-done((bf16[216,640]{1,0:T(8,128)(2,1)S(1)}, bf16[216,640]{1,0:T(8,128)(2,1)S(1)}, u32[]{:S(2)}, u32[]{:S(2)}) %collective-permute-start.14) | collective-permute-done | bytes 276512 | tf_op jit(solution)/shard_map/ppermute | solution.py:216
  141.4 3.6 %collective-permute-start.16 = (bf16[216,640]{1,0:T(8,128)(2,1)}, bf16[216,640]{1,0:T(8,128)(2,1)S(1)}, u32[]{:S(2)}, u32[]{:S(2)}) collective-permute-start(bf16[216,640]{1,0:T(8,128)(2,1)} %get-tuple-element.59), channel_id=1, source_target_pairs={{0,32},{2,34},{4,36},{6,38},{8,40},{10,42},{12,44},{14,46},{16,48}... | collective-permute-start | bytes 829448 | tf_op jit(solution)/shard_map/ppermute | solution.py:216
  145.0 3.6 %collective-permute-start.18 = (bf16[216,640]{1,0:T(8,128)(2,1)S(1)}, bf16[216,640]{1,0:T(8,128)(2,1)S(1)}, u32[]{:S(2)}, u32[]{:S(2)}) collective-permute-start(bf16[216,640]{1,0:T(8,128)(2,1)S(1)} %get-tuple-element.61), channel_id=1, source_target_pairs={{0,48},{2,50},{4,52},{6,54},{8,56},{10,58},{12,60},{14,62},{16,0},... | collective-permute-start | bytes 829448 | tf_op jit(solution)/shard_map/ppermute | solution.py:216
  148.6 4.1 %collective-permute-start.19 = (bf16[216,640]{1,0:T(8,128)(2,1)S(1)}, bf16[216,640]{1,0:T(8,128)(2,1)S(1)}, u32[]{:S(2)}, u32[]{:S(2)}) collective-permute-start(bf16[216,640]{1,0:T(8,128)(2,1)S(1)} %get-tuple-element.62), channel_id=1, source_target_pairs={{0,56},{2,58},{4,60},{6,62},{8,0},{10,2},{12,4},{14,6},{16,8},{18,... | collective-permute-start | bytes 829448 | tf_op jit(solution)/shard_map/ppermute | solution.py:216
  152.7 3.7 %shard_map.122 = (bf16[216,5120]{1,0:T(8,128)(2,1)}, f32[1,216]{1,0:T(1,128)}, bf16[32,5120]{1,0:T(8,128)(2,1)S(1)}, f32[8,4,128]{2,1,0:T(4,128)S(1)}) custom-call(bf16[8,368,128]{2,1,0:T(8,128)(2,1)S(1)} %get-tuple-element.45.refs_0_, bf16[8,368,128]{2,1,0:T(8,128)(2,1)S(1)} %collective-permute-done.7.refs_1_, ...), custom_call_target="tpu_custom_call" | custom-call | tf_op jit(solution)/shard_map/pallas_call | solution.py:244
  156.5 10.8 %collective-permute-done.17.refs_5_ = bf16[216,640]{1,0:T(8,128)(2,1)S(1)} collective-permute-done((bf16[216,640]{1,0:T(8,128)(2,1)S(1)}, bf16[216,640]{1,0:T(8,128)(2,1)S(1)}, u32[]{:S(2)}, u32[]{:S(2)}) %collective-permute-start.17) | collective-permute-done | bytes 276512 | tf_op jit(solution)/shard_map/ppermute | solution.py:216
  167.2 1.8 %collective-permute-done.18.refs_6_ = bf16[216,640]{1,0:T(8,128)(2,1)S(1)} collective-permute-done((bf16[216,640]{1,0:T(8,128)(2,1)S(1)}, bf16[216,640]{1,0:T(8,128)(2,1)S(1)}, u32[]{:S(2)}, u32[]{:S(2)}) %collective-permute-start.18) | collective-permute-done | bytes 276512 | tf_op jit(solution)/shard_map/ppermute | solution.py:216
  169.0 5.6 %collective-permute-done.19.refs_7_ = bf16[216,640]{1,0:T(8,128)(2,1)S(1)} collective-permute-done((bf16[216,640]{1,0:T(8,128)(2,1)S(1)}, bf16[216,640]{1,0:T(8,128)(2,1)S(1)}, u32[]{:S(2)}, u32[]{:S(2)}) %collective-permute-start.19) | collective-permute-done | bytes 276512 | tf_op jit(solution)/shard_map/ppermute | solution.py:216
  174.6 2.7 %shard_map.124 = (bf16[216,5120]{1,0:T(8,128)(2,1)}, f32[1,216]{1,0:T(1,128)}) custom-call(bf16[216,640]{1,0:T(8,128)(2,1)S(1)} %get-tuple-element.55.refs_0_, bf16[216,640]{1,0:T(8,128)(2,1)S(1)} %collective-permute-done.13.refs_1_, bf16[216,640]{1,0:T(8,128)(2,1)S(1)} %collective-permute-done.14.refs_2_, ...), custom_call_target="tpu_custom_call" | custom-call | tf_op jit(solution)/shard_map/pallas_call | solution.py:259
  (37 shorter events, 4.9 us)
Async XLA Ops:
  0.6 1.6 copy-start
  2.3 0.7 copy-start.4
  3.0 0.7 copy-start.5
  3.7 0.7 copy-start.6
  4.3 0.7 copy-start.7
  5.0 3.5 %copy-start.1 = (bf16[160,6912]{1,0:T(8,128)(2,1)S(1)}, bf16[160,6912]{1,0:T(8,128)(2,1)}, u32[]{:S(2)}) copy-start(bf16[160,6912]{1,0:T(8,128)(2,1)} %weight.3) | copy-start | bytes 6635524
  6.5 15.9 %collective-permute-start = (bf16[1168,128]{1,0:T(8,128)(2,1)S(1)}, bf16[1168,128]{1,0:T(8,128)(2,1)S(1)}, u32[]{:S(2)}, u32[]{:S(2)}) collective-permute-start(bf16[1168,128]{1,0:T(8,128)(2,1)S(1)} %get-tuple-element.38), channel_id=1, source_target_pairs={{0,8},{2,10},{4,12},{6,14},{8,16},{10,18},{12,20},{14,22},{16,24},... | collective-permute-start | bytes 897032 | tf_op jit(solution)/shard_map/ppermute | solution.py:216
  8.5 1.0 copy-start.2
  9.5 1.0 copy-start.3
  12.3 70.9 %collective-permute-start.10 = (bf16[8,320,128]{2,1,0:T(8,128)(2,1)S(1)}, bf16[8,320,128]{2,1,0:T(8,128)(2,1)S(1)}, u32[]{:S(2)}, u32[]{:S(2)}) collective-permute-start(bf16[8,320,128]{2,1,0:T(8,128)(2,1)S(1)} %get-tuple-element.52), channel_id=1, source_target_pairs={{0,2},{2,0},{4,6},{6,4},{8,10},{10,8},{12,14},{14,12},{16,18},{18,... | collective-permute-start | bytes 1966088 | tf_op jit(solution)/shard_map/ppermute | solution.py:222
  14.6 21.9 %collective-permute-start.1 = (bf16[1168,128]{1,0:T(8,128)(2,1)S(1)}, bf16[1168,128]{1,0:T(8,128)(2,1)S(1)}, u32[]{:S(2)}, u32[]{:S(2)}) collective-permute-start(bf16[1168,128]{1,0:T(8,128)(2,1)S(1)} %get-tuple-element.39), channel_id=1, source_target_pairs={{0,16},{2,18},{4,20},{6,22},{8,24},{10,26},{12,28},{14,30},{16,32}... | collective-permute-start | bytes 897032 | tf_op jit(solution)/shard_map/ppermute | solution.py:216
  19.0 37.6 %collective-permute-start.2 = (bf16[1168,128]{1,0:T(8,128)(2,1)S(1)}, bf16[1168,128]{1,0:T(8,128)(2,1)S(1)}, u32[]{:S(2)}, u32[]{:S(2)}) collective-permute-start(bf16[1168,128]{1,0:T(8,128)(2,1)S(1)} %get-tuple-element.40), channel_id=1, source_target_pairs={{0,24},{2,26},{4,28},{6,30},{8,32},{10,34},{12,36},{14,38},{16,40}... | collective-permute-start | bytes 897032 | tf_op jit(solution)/shard_map/ppermute | solution.py:216
  21.0 35.7 %collective-permute-start.3 = (bf16[1168,128]{1,0:T(8,128)(2,1)S(1)}, bf16[1168,128]{1,0:T(8,128)(2,1)S(1)}, u32[]{:S(2)}, u32[]{:S(2)}) collective-permute-start(bf16[1168,128]{1,0:T(8,128)(2,1)S(1)} %get-tuple-element.41), channel_id=1, source_target_pairs={{0,32},{2,34},{4,36},{6,38},{8,40},{10,42},{12,44},{14,46},{16,48}... | collective-permute-start | bytes 897032 | tf_op jit(solution)/shard_map/ppermute | solution.py:216
  22.4 37.4 %collective-permute-start.4 = (bf16[1168,128]{1,0:T(8,128)(2,1)S(1)}, bf16[1168,128]{1,0:T(8,128)(2,1)S(1)}, u32[]{:S(2)}, u32[]{:S(2)}) collective-permute-start(bf16[1168,128]{1,0:T(8,128)(2,1)S(1)} %get-tuple-element.42), channel_id=1, source_target_pairs={{0,40},{2,42},{4,44},{6,46},{8,48},{10,50},{12,52},{14,54},{16,56}... | collective-permute-start | bytes 897032 | tf_op jit(solution)/shard_map/ppermute | solution.py:216
  36.5 35.6 %collective-permute-start.5 = (bf16[1168,128]{1,0:T(8,128)(2,1)S(1)}, bf16[1168,128]{1,0:T(8,128)(2,1)S(1)}, u32[]{:S(2)}, u32[]{:S(2)}) collective-permute-start(bf16[1168,128]{1,0:T(8,128)(2,1)S(1)} %get-tuple-element.43), channel_id=1, source_target_pairs={{0,48},{2,50},{4,52},{6,54},{8,56},{10,58},{12,60},{14,62},{16,0},... | collective-permute-start | bytes 897032 | tf_op jit(solution)/shard_map/ppermute | solution.py:216
  56.6 20.0 %collective-permute-start.6 = (bf16[1168,128]{1,0:T(8,128)(2,1)S(1)}, bf16[1168,128]{1,0:T(8,128)(2,1)S(1)}, u32[]{:S(2)}, u32[]{:S(2)}) collective-permute-start(bf16[1168,128]{1,0:T(8,128)(2,1)S(1)} %get-tuple-element.44), channel_id=1, source_target_pairs={{0,56},{2,58},{4,60},{6,62},{8,0},{10,2},{12,4},{14,6},{16,8},{18,... | collective-permute-start | bytes 897032 | tf_op jit(solution)/shard_map/ppermute | solution.py:216
  56.6 28.5 %collective-permute-start.11 = (bf16[8,320,128]{2,1,0:T(8,128)(2,1)S(1)}, bf16[8,320,128]{2,1,0:T(8,128)(2,1)S(1)}, u32[]{:S(2)}, u32[]{:S(2)}) collective-permute-start(bf16[8,320,128]{2,1,0:T(8,128)(2,1)S(1)} %get-tuple-element.53), channel_id=1, source_target_pairs={{0,4},{2,6},{4,0},{6,2},{8,12},{10,14},{12,8},{14,10},{16,20},{18,... | collective-permute-start | bytes 1966088 | tf_op jit(solution)/shard_map/ppermute | solution.py:222
  59.8 25.3 %collective-permute-start.12 = (bf16[8,320,128]{2,1,0:T(8,128)(2,1)S(1)}, bf16[8,320,128]{2,1,0:T(8,128)(2,1)S(1)}, u32[]{:S(2)}, u32[]{:S(2)}) collective-permute-start(bf16[8,320,128]{2,1,0:T(8,128)(2,1)S(1)} %get-tuple-element.54), channel_id=1, source_target_pairs={{0,6},{2,4},{4,2},{6,0},{8,14},{10,12},{12,10},{14,8},{16,22},{18,... | collective-permute-start | bytes 1966088 | tf_op jit(solution)/shard_map/ppermute | solution.py:222
  78.5 66.5 %collective-permute-start.7 = (bf16[8,368,128]{2,1,0:T(8,128)(2,1)S(1)}, bf16[8,368,128]{2,1,0:T(8,128)(2,1)S(1)}, u32[]{:S(2)}, u32[]{:S(2)}) collective-permute-start(bf16[8,368,128]{2,1,0:T(8,128)(2,1)S(1)} %get-tuple-element.46), channel_id=1, source_target_pairs={{0,2},{2,0},{4,6},{6,4},{8,10},{10,8},{12,14},{14,12},{16,18},{18,... | collective-permute-start | bytes 2261000 | tf_op jit(solution)/shard_map/ppermute | solution.py:222
  80.0 65.0 %collective-permute-start.8 = (bf16[8,368,128]{2,1,0:T(8,128)(2,1)S(1)}, bf16[8,368,128]{2,1,0:T(8,128)(2,1)S(1)}, u32[]{:S(2)}, u32[]{:S(2)}) collective-permute-start(bf16[8,368,128]{2,1,0:T(8,128)(2,1)S(1)} %get-tuple-element.47), channel_id=1, source_target_pairs={{0,4},{2,6},{4,0},{6,2},{8,12},{10,14},{12,8},{14,10},{16,20},{18,... | collective-permute-start | bytes 2261000 | tf_op jit(solution)/shard_map/ppermute | solution.py:222
  83.2 65.4 %collective-permute-start.9 = (bf16[8,368,128]{2,1,0:T(8,128)(2,1)S(1)}, bf16[8,368,128]{2,1,0:T(8,128)(2,1)S(1)}, u32[]{:S(2)}, u32[]{:S(2)}) collective-permute-start(bf16[8,368,128]{2,1,0:T(8,128)(2,1)S(1)} %get-tuple-element.48), channel_id=1, source_target_pairs={{0,6},{2,4},{4,2},{6,0},{8,14},{10,12},{12,10},{14,8},{16,22},{18,... | collective-permute-start | bytes 2261000 | tf_op jit(solution)/shard_map/ppermute | solution.py:222
  86.7 26.9 %collective-permute-start.13 = (bf16[216,640]{1,0:T(8,128)(2,1)S(1)}, bf16[216,640]{1,0:T(8,128)(2,1)S(1)}, u32[]{:S(2)}, u32[]{:S(2)}) collective-permute-start(bf16[216,640]{1,0:T(8,128)(2,1)S(1)} %get-tuple-element.56), channel_id=1, source_target_pairs={{0,8},{2,10},{4,12},{6,14},{8,16},{10,18},{12,20},{14,22},{16,24},... | collective-permute-start | bytes 829448 | tf_op jit(solution)/shard_map/ppermute | solution.py:216
  101.4 40.0 %collective-permute-start.14 = (bf16[216,640]{1,0:T(8,128)(2,1)S(1)}, bf16[216,640]{1,0:T(8,128)(2,1)S(1)}, u32[]{:S(2)}, u32[]{:S(2)}) collective-permute-start(bf16[216,640]{1,0:T(8,128)(2,1)S(1)} %get-tuple-element.57), channel_id=1, source_target_pairs={{0,16},{2,18},{4,20},{6,22},{8,24},{10,26},{12,28},{14,30},{16,32}... | collective-permute-start | bytes 829448 | tf_op jit(solution)/shard_map/ppermute | solution.py:216
  113.6 42.7 %collective-permute-start.15 = (bf16[216,640]{1,0:T(8,128)(2,1)S(1)}, bf16[216,640]{1,0:T(8,128)(2,1)S(1)}, u32[]{:S(2)}, u32[]{:S(2)}) collective-permute-start(bf16[216,640]{1,0:T(8,128)(2,1)S(1)} %get-tuple-element.58), channel_id=1, source_target_pairs={{0,24},{2,26},{4,28},{6,30},{8,32},{10,34},{12,36},{14,38},{16,40}... | collective-permute-start | bytes 829448 | tf_op jit(solution)/shard_map/ppermute | solution.py:216
  141.4 15.1 %collective-permute-start.16 = (bf16[216,640]{1,0:T(8,128)(2,1)}, bf16[216,640]{1,0:T(8,128)(2,1)S(1)}, u32[]{:S(2)}, u32[]{:S(2)}) collective-permute-start(bf16[216,640]{1,0:T(8,128)(2,1)} %get-tuple-element.59), channel_id=1, source_target_pairs={{0,32},{2,34},{4,36},{6,38},{8,40},{10,42},{12,44},{14,46},{16,48}... | collective-permute-start | bytes 829448 | tf_op jit(solution)/shard_map/ppermute | solution.py:216
  145.0 22.2 %collective-permute-start.17 = (bf16[216,640]{1,0:T(8,128)(2,1)S(1)}, bf16[216,640]{1,0:T(8,128)(2,1)S(1)}, u32[]{:S(2)}, u32[]{:S(2)}) collective-permute-start(bf16[216,640]{1,0:T(8,128)(2,1)S(1)} %get-tuple-element.60), channel_id=1, source_target_pairs={{0,40},{2,42},{4,44},{6,46},{8,48},{10,50},{12,52},{14,54},{16,56}... | collective-permute-start | bytes 829448 | tf_op jit(solution)/shard_map/ppermute | solution.py:216
  145.0 24.0 %collective-permute-start.18 = (bf16[216,640]{1,0:T(8,128)(2,1)S(1)}, bf16[216,640]{1,0:T(8,128)(2,1)S(1)}, u32[]{:S(2)}, u32[]{:S(2)}) collective-permute-start(bf16[216,640]{1,0:T(8,128)(2,1)S(1)} %get-tuple-element.61), channel_id=1, source_target_pairs={{0,48},{2,50},{4,52},{6,54},{8,56},{10,58},{12,60},{14,62},{16,0},... | collective-permute-start | bytes 829448 | tf_op jit(solution)/shard_map/ppermute | solution.py:216
  148.6 26.1 %collective-permute-start.19 = (bf16[216,640]{1,0:T(8,128)(2,1)S(1)}, bf16[216,640]{1,0:T(8,128)(2,1)S(1)}, u32[]{:S(2)}, u32[]{:S(2)}) collective-permute-start(bf16[216,640]{1,0:T(8,128)(2,1)S(1)} %get-tuple-element.62), channel_id=1, source_target_pairs={{0,56},{2,58},{4,60},{6,62},{8,0},{10,2},{12,4},{14,6},{16,8},{18,... | collective-permute-start | bytes 829448 | tf_op jit(solution)/shard_map/ppermute | solution.py:216
  156.4 21.0 %collective-permute-start.20 = (bf16[32,80]{1,0:T(8,128)(2,1)S(1)}, bf16[32,80]{1,0:T(8,128)(2,1)S(1)}, u32[]{:S(2)}, u32[]{:S(2)}) collective-permute-start(bf16[32,80]{1,0:T(8,128)(2,1)S(1)} %bitcast.18), channel_id=1, source_target_pairs={{0,1},{1,0},{2,3},{3,2},{4,5},{5,4},{6,7},{7,6},{8,9},{9,8},{10,11... | collective-permute-start | bytes 15368 | tf_op jit(solution)/shard_map/ppermute | solution.py:254

commit v3 on v2

v3 whole, which is shorter than its diff:
```python
import jax
import jax.numpy as jnp
from jax import lax
from jax.experimental import pallas as pl
from jax.experimental.pallas import tpu as pltpu
from jax.sharding import PartitionSpec as P


D_MODEL = 5120
MIX = 0.5
NZ = 8
NQ = 4
ROWS = 160
COLS = 216
RANK = 32
SPAN = NQ * COLS
TILES = 7
EXTRA = 48
BLOCK = TILES * ROWS + EXTRA
PART = 2 * ROWS + EXTRA
LAST = 51

FIRST = (4,)
EARLY = (1, 7)
LATE = (2, 6, 3, 5)
UP = (4, 3, 5, 2, 6, 1, 7)
NEAR = (0, 1, 7, 2, 6)
FAR = (4, 3, 5)
ORDER = NEAR + FAR
bf16, f32 = jnp.bfloat16, jnp.float32


def lanes(shape):
    return lax.broadcasted_iota(jnp.int32, shape, len(shape) - 1)


def rows(shape):
    return lax.broadcasted_iota(jnp.int32, shape, len(shape) - 2)


def place_t(low_t, period, first):
    shape = (RANK, 128)
    hit = (lanes(shape) >= first) & ((lanes(shape) - first) % period == rows(shape))
    return lax.dot_general(
        low_t, hit.astype(bf16), (((0,), (0,)), ((), ())), preferred_element_type=f32
    )


def window_of(shift):
    start = SPAN * ((lax.axis_index("zero") // NQ + shift) % NZ)
    tile = jnp.minimum(start // 128, LAST - 5)
    return pl.multiple_of(tile * 128, 128), start - 128 * tile


def fetch(weight, windows, sem, shifts):
    copies = []
    for i, k in enumerate(shifts):
        at, _ = window_of(k)
        copies.append(
            pltpu.make_async_copy(weight.at[:, pl.ds(at, 1024)], windows.at[i], sem.at[i])
        )
        copies[i].start()
    return copies


def pack_block(x, shift, low, extra, out):
    _, off = window_of(shift)
    x = pltpu.roll(x.astype(f32), (1024 - off) % 1024, 1)
    for j in range(TILES):
        y = x[:, 128 * j : 128 * j + 128]
        if j == TILES - 1:
            y = jnp.where(lanes((ROWS, 128)) < 96, y, low)
        out[ROWS * j : ROWS * j + ROWS, :] = y.astype(bf16)
    out[ROWS * TILES : BLOCK, :] = extra


def pack_first(weight, low_gate, low_up, train, step, out, tail, windows, lows, norms, sem, small):
    copies = fetch(weight, windows, sem, FIRST)
    others = [
        pltpu.make_async_copy(source, target, small.at[i])
        for i, (source, target) in enumerate(
            ((low_gate, lows.at[0]), (low_up, lows.at[1]), (train, norms.at[0]), (step, norms.at[1]))
        )
    ]
    for copy in others:
        copy.start()
    for copy in others:
        copy.wait()
    low_g = place_t(lows[0], 128, 96)
    low_u = place_t(lows[1], 32, 0)
    group = lanes((40, 128)) // 32
    packed = jnp.zeros((40, 128), f32)
    for g in range(4):
        packed = jnp.where(group == g, low_u[40 * g : 40 * g + 40], packed)
    norm = jnp.concatenate([norms[0] + norms[1], jnp.zeros((1, 48), f32)], axis=1)
    norm = jnp.broadcast_to(norm, (8, 128))
    extra = jnp.concatenate([packed, norm], axis=0).astype(bf16)
    tail[0:ROWS, :] = low_g.astype(bf16)
    tail[ROWS : ROWS + EXTRA, :] = extra
    copies[0].wait()
    pack_block(windows[0], FIRST[0], low_g, extra, out)


def pack_rest(weight, tail, *refs):
    shifts = (*EARLY, *LATE, 0)
    outs, windows, sem = refs[: len(shifts)], refs[-2], refs[-1]
    copies = fetch(weight, windows, sem, shifts)
    low = tail[0:ROWS, :].astype(f32)
    extra = tail[ROWS : ROWS + EXTRA, :]
    for i, k in enumerate(shifts):
        copies[i].wait()
        pack_block(windows[i], k, low, extra, outs[i])


def window(x, off):
    return pltpu.roll(x, (384 - off) % 384, 1)[:, :256]


def pack_up(weight, *parts):
    q = lax.axis_index("zero") % NQ
    for p in range(NQ):
        for z in range(NZ):
            start = COLS * (z * NQ + jnp.bitwise_xor(q, p))
            tile = jnp.minimum(start // 128, LAST)
            x = weight[:, pl.ds(pl.multiple_of(tile * 128, 128), 384)].astype(f32)
            x = window(x, start - 128 * tile)
            parts[p][z, 0:ROWS, :] = x[:, :128].astype(bf16)
            parts[p][z, ROWS : 2 * ROWS, :] = x[:, 128:].astype(bf16)


def turn_high(high_gate, high_up, mix, high, highs, sem):
    start = COLS * lax.axis_index("zero")
    tile = jnp.minimum(start // 128, LAST)
    own = pl.ds(pl.multiple_of(tile * 128, 128), 384)
    copies = [
        pltpu.make_async_copy(source.at[:, own], highs.at[i], sem.at[i])
        for i, source in enumerate((high_gate, high_up))
    ]
    for copy in copies:
        copy.start()
    for copy in copies:
        copy.wait()

    def own_high(i):
        x = pltpu.roll(highs[i].astype(f32), (384 - (start - 128 * tile)) % 384, 1)
        return x[:, :256].astype(bf16)

    def turned(h, first, width):
        shape = (RANK, width)
        hit = jnp.where(lanes(shape) == rows(shape) + first, MIX, 0.0).astype(bf16)
        return lax.dot_general(h, hit, (((0,), (0,)), ((), ())), preferred_element_type=f32)

    eye = (lanes((256, 256)) == rows((256, 256))) & (rows((256, 256)) < COLS)
    mix[...] = (eye.astype(f32) + turned(own_high(0), COLS, 256)).astype(bf16)
    high[...] = turned(own_high(1), 0, 128).astype(bf16)


def turn_up(*refs):
    parts, outs, x = refs[:NQ], refs[NQ : NQ + NZ], refs[NQ + NZ]
    place = lax.axis_index("zero")
    q, here = place % NQ, place // NQ
    eye = (lanes((COLS, 256)) == rows((COLS, 256))).astype(bf16)
    for k in (*UP, 0):
        z = (here + k) % NZ
        for p in range(NQ):
            at = pl.multiple_of(jnp.bitwise_xor(q, p) * ROWS, ROWS)
            x[k % 2, pl.ds(at, ROWS), 0:128] = parts[p][z, 0:ROWS, :]
            x[k % 2, pl.ds(at, ROWS), 128:256] = parts[p][z, ROWS : 2 * ROWS, :]
        outs[k][...] = lax.dot_general(
            eye, x[k % 2], (((1,), (1,)), ((), ())), preferred_element_type=f32
        ).astype(bf16)


def split_gate(*refs):
    count = len(refs) - NQ
    blocks, parts = refs[:count], refs[count:]
    q = lax.axis_index("zero") % NQ
    wide = (ROWS, 128)
    for i, block in enumerate(blocks):
        low = pltpu.roll(block[ROWS * 6 : ROWS * 7, :].astype(f32), 120, 1)
        for p in range(NQ):
            start = COLS * jnp.bitwise_xor(q, p)
            tile = jnp.minimum(start // 128, TILES - 3)
            x = jnp.concatenate(
                [
                    block[pl.ds(pl.multiple_of((tile + n) * ROWS, ROWS), ROWS), :].astype(f32)
                    for n in range(3)
                ],
                axis=1,
            )
            x = window(x, start - 128 * tile)
            last = jnp.where(lanes(wide) < 88, x[:, 128:], jnp.where(lanes(wide) < 120, low, 0.0))
            parts[p][i, 0:ROWS, :] = x[:, :128].astype(bf16)
            parts[p][i, ROWS : 2 * ROWS, :] = last.astype(bf16)
            parts[p][i, 2 * ROWS : PART, :] = block[ROWS * TILES : BLOCK, :]


def scales(total):
    column = jnp.sum(total, axis=1, keepdims=True) / D_MODEL
    padded = jnp.concatenate([total, jnp.zeros((256 - COLS, 128), f32)], axis=0)
    row = jnp.sum(jnp.transpose(padded), axis=0, keepdims=True) / D_MODEL
    return column, row[:, :COLS]


def magnitudes(r):
    a = jnp.abs(r)
    return sum(a[:, 128 * k : 128 * k + 128] for k in range(5))


def norm_rows(*refs):
    place = lax.axis_index("zero")
    q, here = place % NQ, place // NQ
    for i, k in enumerate(ORDER):
        z = (here + NZ - k) % NZ
        half, j = (0, i) if i < len(NEAR) else (1, i - len(NEAR))
        for p in range(NQ):
            extra = refs[NQ * half + p][j, 2 * ROWS : PART, :].astype(f32)
            refs[2 * NQ][pl.ds(NQ * z + jnp.bitwise_xor(q, p), 1), :] = extra[40:41]


def norm_join(mine, other, out):
    first = 80 * lax.axis_index("cols")
    total = jnp.zeros((40, 128), f32)
    for source, start in ((mine, first), (other, 80 - first)):
        values = source[...].astype(bf16)
        for j in range(5):
            for m in range(NQ):
                if 160 * m >= 128 * (j + 1) or 160 * (m + 1) <= 128 * j:
                    continue
                shape = (40, NZ * NQ)
                at = rows(shape)
                row = (at % 5 == j) & (lanes(shape) == at // 5 * NQ + m)
                picked = jnp.dot(row.astype(bf16), values, preferred_element_type=f32)
                shape = (128, 128)
                lane = (rows(shape) < 80) & (rows(shape) + start + 160 * m == lanes(shape) + 128 * j)
                total = total + jnp.dot(
                    picked.astype(bf16), lane.astype(bf16), preferred_element_type=f32
                )
    out[...] = total.astype(bf16)


def last_gate(*refs):
    near, far, (mix, out, scale, low) = refs[:NQ], refs[NQ : 2 * NQ], refs[2 * NQ : 2 * NQ + 4]
    x, lows, sums = refs[2 * NQ + 4 :]
    place = lax.axis_index("zero")
    q, here = place % NQ, place // NQ
    total = jnp.zeros((COLS, 128), f32)
    m = mix[0:COLS, :]
    pick = (lanes((RANK, 128)) == rows((RANK, 128))).astype(bf16)
    turned = (((1,), (1,)), ((), ()))
    for i, k in enumerate(ORDER):
        parts, j = (near, i) if i < len(NEAR) else (far, i - len(NEAR))
        for p in range(NQ):
            at = pl.multiple_of(jnp.bitwise_xor(q, p) * ROWS, ROWS)
            x[i % 2, pl.ds(at, ROWS), 0:128] = parts[p][j, 0:ROWS, :]
            x[i % 2, pl.ds(at, ROWS), 128:256] = parts[p][j, ROWS : 2 * ROWS, :]
            extra = parts[p][j, 2 * ROWS : PART, :].astype(f32)[0:40]
            wide = jnp.concatenate(
                [pltpu.roll(extra, (128 - 32 * g) % 128, 1) for g in range(4)], axis=0
            )
            lows[i % 2, pl.ds(at, ROWS), :] = wide.astype(bf16)
        at = pl.multiple_of((here + NZ - k) % NZ * 640, 640)
        r = lax.dot_general(m, x[i % 2], turned, preferred_element_type=f32)
        sums[:, pl.ds(at, 640)] = r
        total = total + magnitudes(r)
        low[:, pl.ds(at, 640)] = lax.dot_general(
            pick, lows[i % 2], turned, preferred_element_type=f32
        ).astype(bf16)
    column, row = scales(total)
    scale[...] = row
    out[...] = (sums[...] * (1.0 / column)).astype(bf16)


def last_up(*refs):
    blocks, high, low = refs[:NZ], refs[NZ], refs[NZ + 1]
    out, scale, sums = refs[NZ + 3 :]
    here = lax.axis_index("zero") // NQ
    total = jnp.zeros((COLS, 128), f32)
    h = high[0:COLS, 0:RANK]
    for k in range(NZ):
        at = pl.multiple_of((here + NZ - k) % NZ * 640, 640)
        r = blocks[k][...].astype(f32) + jnp.dot(
            h, low[:, pl.ds(at, 640)], preferred_element_type=f32
        )
        sums[:, pl.ds(at, 640)] = r
        total = total + magnitudes(r)
    column, row = scales(total)
    scale[...] = row
    out[...] = (sums[...] * (1.0 / column)).astype(bf16)


HBM, VMEM = pl.BlockSpec(memory_space=pltpu.HBM), pl.BlockSpec(memory_space=pltpu.VMEM)


def kernel(body, outs, scratch=(), ins=None, places=None):
    specs = {} if ins is None else {"in_specs": ins}
    if places is not None:
        specs["out_specs"] = places
    return pl.pallas_call(
        body,
        out_shape=[jax.ShapeDtypeStruct(*o) for o in outs],
        scratch_shapes=list(scratch),
        compiler_params=pltpu.CompilerParams(vmem_limit_bytes=24 * 2**20),
        **specs,
    )


def hbm(x):
    return pltpu.with_memory_space_constraint(x, pltpu.HBM)


def along_z(block, shift):
    pairs = [(z * NQ + q, (z + shift) % NZ * NQ + q) for z in range(NZ) for q in range(NQ)]
    return lax.ppermute(block, "zero", pairs)


def across(parts):
    moved = [
        lax.ppermute(part, "zero", [(s, s ^ p) for s in range(NZ * NQ)])
        for p, part in enumerate(parts)
        if p
    ]
    return [parts[0], *moved]


def local(weight_gate, low_gate, high_gate, weight_up, low_up, high_up, norm_train, norm_step):
    dma = pltpu.SemaphoreType.DMA
    inward = {}
    first, tail = kernel(
        pack_first,
        [((BLOCK, 128), bf16), ((ROWS + EXTRA, 128), bf16)],
        [
            pltpu.VMEM((1, ROWS, 1024), bf16),
            pltpu.VMEM((2, RANK, ROWS), bf16),
            pltpu.VMEM((2, 1, 80), f32),
            dma((1,)),
            dma((4,)),
        ],
        [HBM] * 5,
    )(*map(hbm, (weight_gate, low_gate.T, low_up.T, norm_train[None], norm_step[None])))
    inward[FIRST[0]] = along_z(first, FIRST[0])
    shifts = (*EARLY, *LATE, 0)
    blocks = kernel(
        pack_rest,
        [((BLOCK, 128), bf16)] * len(shifts),
        [pltpu.VMEM((len(shifts), ROWS, 1024), bf16), dma((len(shifts),))],
        [HBM, VMEM],
    )(hbm(weight_gate), tail)
    for k, block in zip(shifts, blocks):
        inward[k] = along_z(block, k) if k else block
    up_parts = kernel(pack_up, [((NZ, 2 * ROWS, 128), bf16)] * NQ)(weight_up)
    up_parts = across(up_parts)
    up_blocks = kernel(
        turn_up, [((COLS, 640), bf16)] * NZ, [pltpu.VMEM((2, NQ * ROWS, 256), bf16)]
    )(*up_parts)
    up_in = list(up_blocks)
    for k in UP:
        up_in[k] = along_z(up_blocks[k], k)
    halves = []
    for shifts in (NEAR, FAR):
        parts = kernel(
            split_gate, [((len(shifts), PART, 128), bf16)] * NQ
        )(*[inward[k] for k in shifts])
        halves.append(across(parts))
    mix, high = kernel(
        turn_high,
        [((256, 256), bf16), ((256, 128), bf16)],
        [pltpu.VMEM((2, RANK, 384), bf16), dma((2,))],
        [HBM, HBM],
    )(hbm(high_gate), hbm(high_up))
    (norm,) = kernel(norm_rows, [((NZ * NQ, 128), f32)])(*halves[0], *halves[1])
    final_gate, scale_gate, low = kernel(
        last_gate,
        [((COLS, D_MODEL), bf16), ((1, COLS), f32), ((RANK, D_MODEL), bf16)],
        [
            pltpu.VMEM((2, NQ * ROWS, 256), bf16),
            pltpu.VMEM((2, NQ * ROWS, 128), bf16),
            pltpu.VMEM((COLS, D_MODEL), f32),
        ],
    )(*halves[0], *halves[1], mix)
    other = lax.ppermute(norm, "cols", [(0, 1), (1, 0)])
    (serve_norm,) = kernel(norm_join, [((40, 128), bf16)])(norm, other)
    final_up, scale_up = kernel(
        last_up,
        [((COLS, D_MODEL), bf16), ((1, COLS), f32)],
        [pltpu.VMEM((COLS, D_MODEL), f32)],
        [VMEM] * (NZ + 2) + [HBM],
    )(*up_in, high, low, hbm(serve_norm))
    return (final_gate.T, final_up.T, scale_gate[0], scale_up[0], serve_norm.reshape(D_MODEL))


def solution(mesh):
    in_specs = (
        P(("unit", "zero"), "cols"),
        P(("unit", "zero"), None),
        P("unit", "cols"),
        P(("unit", "zero"), "cols"),
        P(("unit", "zero"), None),
        P("unit", "cols"),
        P(("unit", "zero", "cols")),
        P(("unit", "zero", "cols")),
    )
    out_specs = (
        P("unit", ("cols", "zero")),
        P("unit", ("cols", "zero")),
        P(("unit", "cols", "zero")),
        P(("unit", "cols", "zero")),
        P("unit"),
    )
    return jax.shard_map(local, mesh=mesh, in_specs=in_specs, out_specs=out_specs, check_vma=False)
```

time: 178 us -> 163 us (0.916)
  the two profiles are of different devices: /device:TPU:34 before, /device:TPU:6 now
where the time goes in v3:
time: 163 us; the launch traced here: 162 us
  waiting for transfers between devices  84.2 us (52%)
  starting transfers between devices  59.4 us (36%)
  Pallas kernels  18 us (11%)
    ppermute x14, waiting for transfers between devices, along_z(): return lax.ppermute(block, 'zero', pairs)  63.9 us
    ppermute x14, starting transfers between devices, along_z(): return lax.ppermute(block, 'zero', pairs)  37.5 us
    ppermute x9, starting transfers between devices, across(): lax.ppermute(part, 'zero', [(s, s ^ p) for s in range(NZ * NQ)])  21 us
    ppermute x9, waiting for transfers between devices, across(): lax.ppermute(part, 'zero', [(s, s ^ p) for s in range(NZ * NQ)])  20.3 us
    pallas_call x1, Pallas kernels, local(): kernel(last_gate, [((COLS, D_MODEL), bf16), ((1, COLS), f32), ((RANK, D_M...  3.95 us
  transfers between devices with their start and end apart: 24, of which 13 were waited for; matrix products, arithmetic and copies ran while one was open for 0% of the time, Pallas kernels for 9%

profile of v3, /device:TPU:6, one launch (start us, length us, event | category | flops | bytes accessed | tf_op | source)
XLA Modules:
  0.0 162.4 jit_solution(5227650796457847992)
XLA Ops:
  0.6 1.5 shard_map.119
  2.1 7.3 %collective-permute-start.7 = (bf16[1168,128]{1,0:T(8,128)(2,1)S(1)}, bf16[1168,128]{1,0:T(8,128)(2,1)S(1)}, u32[]{:S(2)}, u32[]{:S(2)}) collective-permute-start(bf16[1168,128]{1,0:T(8,128)(2,1)S(1)} %get-tuple-element.51), channel_id=1, source_target_pairs={{0,32},{2,34},{4,36},{6,38},{8,40},{10,42},{12,44},{14,46},{16,48}... | collective-permute-start | bytes 897032 | tf_op jit(solution)/shard_map/ppermute | solution.py:314
  9.4 2.7 %shard_map.120 = (bf16[1168,128]{1,0:T(8,128)(2,1)S(1)}, bf16[1168,128]{1,0:T(8,128)(2,1)S(1)}, bf16[1168,128]{1,0:T(8,128)(2,1)S(1)}, bf16[1168,128]{1,0:T(8,12...) custom-call(bf16[160,6912]{1,0:T(8,128)(2,1)} %weight.4, ...), custom_call_target="tpu_custom_call" | custom-call | tf_op jit(solution)/shard_map/pallas_call | solution.py:343
  13.2 2.2 %collective-permute-start.1 = (bf16[1168,128]{1,0:T(8,128)(2,1)S(1)}, bf16[1168,128]{1,0:T(8,128)(2,1)S(1)}, u32[]{:S(2)}, u32[]{:S(2)}) collective-permute-start(bf16[1168,128]{1,0:T(8,128)(2,1)S(1)} %get-tuple-element.44), channel_id=1, source_target_pairs={{0,56},{2,58},{4,60},{6,62},{8,0},{10,2},{12,4},{14,6},{16,8},{18,... | collective-permute-start | bytes 897032 | tf_op jit(solution)/shard_map/ppermute | solution.py:314
  16.2 4.3 %collective-permute-start.9 = (bf16[1168,128]{1,0:T(8,128)(2,1)S(1)}, bf16[1168,128]{1,0:T(8,128)(2,1)S(1)}, u32[]{:S(2)}, u32[]{:S(2)}) collective-permute-start(bf16[1168,128]{1,0:T(8,128)(2,1)S(1)} %get-tuple-element.53), channel_id=1, source_target_pairs={{0,40},{2,42},{4,44},{6,46},{8,48},{10,50},{12,52},{14,54},{16,56}... | collective-permute-start | bytes 897032 | tf_op jit(solution)/shard_map/ppermute | solution.py:314
  20.5 1.7 %shard_map.125 = (bf16[8,320,128]{2,1,0:T(8,128)(2,1)S(1)}, bf16[8,320,128]{2,1,0:T(8,128)(2,1)S(1)}, bf16[8,320,128]{2,1,0:T(8,128)(2,1)S(1)}, bf16[8,320,128]{2,1,0:T(8,128)(2,1)S(1)}) custom-call(bf16[160,6912]{1,0:T(8,128)(2,1)S(1)} %copy-done), custom_call_target="tpu_custom_call" | custom-call | tf_op jit(solution)/shard_map/pallas_call | solution.py:351
  22.5 1.4 collective-permute-start.13
  23.9 10.3 %collective-permute-done.refs_1_ = bf16[1168,128]{1,0:T(8,128)(2,1)S(1)} collective-permute-done((bf16[1168,128]{1,0:T(8,128)(2,1)S(1)}, bf16[1168,128]{1,0:T(8,128)(2,1)S(1)}, u32[]{:S(2)}, u32[]{:S(2)}) %collective-permute-start) | collective-permute-done | bytes 299040 | tf_op jit(solution)/shard_map/ppermute | solution.py:314
  34.2 3.2 %collective-permute-start.14 = (bf16[8,320,128]{2,1,0:T(8,128)(2,1)S(1)}, bf16[8,320,128]{2,1,0:T(8,128)(2,1)S(1)}, u32[]{:S(2)}, u32[]{:S(2)}) collective-permute-start(bf16[8,320,128]{2,1,0:T(8,128)(2,1)S(1)} %get-tuple-element.62), channel_id=1, source_target_pairs={{0,4},{2,6},{4,0},{6,2},{8,12},{10,14},{12,8},{14,10},{16,20},{18,... | collective-permute-start | bytes 1966088 | tf_op jit(solution)/shard_map/ppermute | solution.py:319
  38.5 7.9 %collective-permute-done.8.refs_1_ = bf16[1168,128]{1,0:T(8,128)(2,1)S(1)} collective-permute-done((bf16[1168,128]{1,0:T(8,128)(2,1)S(1)}, bf16[1168,128]{1,0:T(8,128)(2,1)S(1)}, u32[]{:S(2)}, u32[]{:S(2)}) %collective-permute-start.8) | collective-permute-done | bytes 299040 | tf_op jit(solution)/shard_map/ppermute | solution.py:314
  46.4 1.5 collective-permute-start.2
  47.9 1.3 collective-permute-done.9.refs_2_
  49.2 3.7 %collective-permute-start.3 = (bf16[1168,128]{1,0:T(8,128)(2,1)S(1)}, bf16[1168,128]{1,0:T(8,128)(2,1)S(1)}, u32[]{:S(2)}, u32[]{:S(2)}) collective-permute-start(bf16[1168,128]{1,0:T(8,128)(2,1)S(1)} %get-tuple-element.46), channel_id=1, source_target_pairs={{0,48},{2,50},{4,52},{6,54},{8,56},{10,58},{12,60},{14,62},{16,0},... | collective-permute-start | bytes 897032 | tf_op jit(solution)/shard_map/ppermute | solution.py:314
  53.6 9.2 %collective-permute-done.2.refs_3_ = bf16[1168,128]{1,0:T(8,128)(2,1)S(1)} collective-permute-done((bf16[1168,128]{1,0:T(8,128)(2,1)S(1)}, bf16[1168,128]{1,0:T(8,128)(2,1)S(1)}, u32[]{:S(2)}, u32[]{:S(2)}) %collective-permute-start.2) | collective-permute-done | bytes 299040 | tf_op jit(solution)/shard_map/ppermute | solution.py:314
  62.8 1.4 collective-permute-start.10
  64.7 3.2 %collective-permute-start.11 = (bf16[3,368,128]{2,1,0:T(8,128)(2,1)S(1)}, bf16[3,368,128]{2,1,0:T(8,128)(2,1)S(1)}, u32[]{:S(2)}, u32[]{:S(2)}) collective-permute-start(bf16[3,368,128]{2,1,0:T(8,128)(2,1)S(1)} %get-tuple-element.56), channel_id=1, source_target_pairs={{0,4},{2,6},{4,0},{6,2},{8,12},{10,14},{12,8},{14,10},{16,20},{18,... | collective-permute-start | bytes 847880 | tf_op jit(solution)/shard_map/ppermute | solution.py:319
  67.9 5.1 %collective-permute-done.10.refs_5_ = bf16[3,368,128]{2,1,0:T(8,128)(2,1)S(1)} collective-permute-done((bf16[3,368,128]{2,1,0:T(8,128)(2,1)S(1)}, bf16[3,368,128]{2,1,0:T(8,128)(2,1)S(1)}, u32[]{:S(2)}, u32[]{:S(2)}) %collective-permute-start.10) | collective-permute-done | bytes 282656 | tf_op jit(solution)/shard_map/ppermute | solution.py:319
  73.0 4.0 %collective-permute-start.12 = (bf16[3,368,128]{2,1,0:T(8,128)(2,1)S(1)}, bf16[3,368,128]{2,1,0:T(8,128)(2,1)S(1)}, u32[]{:S(2)}, u32[]{:S(2)}) collective-permute-start(bf16[3,368,128]{2,1,0:T(8,128)(2,1)S(1)} %get-tuple-element.57), channel_id=1, source_target_pairs={{0,6},{2,4},{4,2},{6,0},{8,14},{10,12},{12,10},{14,8},{16,22},{18,... | collective-permute-start | bytes 847880 | tf_op jit(solution)/shard_map/ppermute | solution.py:319
  78.2 2.2 %collective-permute-start.4 = (bf16[5,368,128]{2,1,0:T(8,128)(2,1)S(1)}, bf16[5,368,128]{2,1,0:T(8,128)(2,1)S(1)}, u32[]{:S(2)}, u32[]{:S(2)}) collective-permute-start(bf16[5,368,128]{2,1,0:T(8,128)(2,1)S(1)} %get-tuple-element.48), channel_id=1, source_target_pairs={{0,2},{2,0},{4,6},{6,4},{8,10},{10,8},{12,14},{14,12},{16,18},{18,... | collective-permute-start | bytes 1413128 | tf_op jit(solution)/shard_map/ppermute | solution.py:319
  80.8 4.0 %collective-permute-start.6 = (bf16[5,368,128]{2,1,0:T(8,128)(2,1)S(1)}, bf16[5,368,128]{2,1,0:T(8,128)(2,1)S(1)}, u32[]{:S(2)}, u32[]{:S(2)}) collective-permute-start(bf16[5,368,128]{2,1,0:T(8,128)(2,1)S(1)} %get-tuple-element.50), channel_id=1, source_target_pairs={{0,6},{2,4},{4,2},{6,0},{8,14},{10,12},{12,10},{14,8},{16,22},{18,... | collective-permute-start | bytes 1413128 | tf_op jit(solution)/shard_map/ppermute | solution.py:319
  84.8 1.2 shard_map.126
  86.0 3.7 %collective-permute-start.16 = (bf16[216,640]{1,0:T(8,128)(2,1)S(1)}, bf16[216,640]{1,0:T(8,128)(2,1)S(1)}, u32[]{:S(2)}, u32[]{:S(2)}) collective-permute-start(bf16[216,640]{1,0:T(8,128)(2,1)S(1)} %get-tuple-element.65), channel_id=1, source_target_pairs={{0,8},{2,10},{4,12},{6,14},{8,16},{10,18},{12,20},{14,22},{16,24},... | collective-permute-start | bytes 829448 | tf_op jit(solution)/shard_map/ppermute | solution.py:314
  89.8 7.0 %collective-permute-done.4.refs_1_ = bf16[5,368,128]{2,1,0:T(8,128)(2,1)S(1)} collective-permute-done((bf16[5,368,128]{2,1,0:T(8,128)(2,1)S(1)}, bf16[5,368,128]{2,1,0:T(8,128)(2,1)S(1)}, u32[]{:S(2)}, u32[]{:S(2)}) %collective-permute-start.4) | collective-permute-done | bytes 471072 | tf_op jit(solution)/shard_map/ppermute | solution.py:319
  96.8 8.2 %collective-permute-done.5.refs_2_ = bf16[5,368,128]{2,1,0:T(8,128)(2,1)S(1)} collective-permute-done((bf16[5,368,128]{2,1,0:T(8,128)(2,1)S(1)}, bf16[5,368,128]{2,1,0:T(8,128)(2,1)S(1)}, u32[]{:S(2)}, u32[]{:S(2)}) %collective-permute-start.5) | collective-permute-done | bytes 471072 | tf_op jit(solution)/shard_map/ppermute | solution.py:319
  107.2 6.1 %collective-permute-start.19 = (bf16[216,640]{1,0:T(8,128)(2,1)S(1)}, bf16[216,640]{1,0:T(8,128)(2,1)S(1)}, u32[]{:S(2)}, u32[]{:S(2)}) collective-permute-start(bf16[216,640]{1,0:T(8,128)(2,1)S(1)} %get-tuple-element.68), channel_id=1, source_target_pairs={{0,32},{2,34},{4,36},{6,38},{8,40},{10,42},{12,44},{14,46},{16,48}... | collective-permute-start | bytes 829448 | tf_op jit(solution)/shard_map/ppermute | solution.py:314
  113.3 5.0 %collective-permute-start.20 = (bf16[216,640]{1,0:T(8,128)(2,1)S(1)}, bf16[216,640]{1,0:T(8,128)(2,1)S(1)}, u32[]{:S(2)}, u32[]{:S(2)}) collective-permute-start(bf16[216,640]{1,0:T(8,128)(2,1)S(1)} %get-tuple-element.69), channel_id=1, source_target_pairs={{0,40},{2,42},{4,44},{6,46},{8,48},{10,50},{12,52},{14,54},{16,56}... | collective-permute-start | bytes 829448 | tf_op jit(solution)/shard_map/ppermute | solution.py:314
  120.1 4.0 %shard_map.124 = (bf16[216,5120]{1,0:T(8,128)(2,1)}, f32[1,216]{1,0:T(1,128)}, bf16[32,5120]{1,0:T(8,128)(2,1)S(1)}) custom-call(bf16[5,368,128]{2,1,0:T(8,128)(2,1)S(1)} %get-tuple-element.47.refs_0_, bf16[5,368,128]{2,1,0:T(8,128)(2,1)S(1)} %collective-permute-done.4.refs_1_, bf16[5,368,128]{2,1,0:T(8,128)(2,1)S(1)} %collective-permute-done.5.refs_2_, ...), custom_call_target="tpu_custom_call" | custom-call | tf_op jit(solution)/shard_map/pallas_call | solution.py:372
  125.2 16.5 %collective-permute-done.19.refs_4_ = bf16[216,640]{1,0:T(8,128)(2,1)S(1)} collective-permute-done((bf16[216,640]{1,0:T(8,128)(2,1)S(1)}, bf16[216,640]{1,0:T(8,128)(2,1)S(1)}, u32[]{:S(2)}, u32[]{:S(2)}) %collective-permute-start.19) | collective-permute-done | bytes 276512 | tf_op jit(solution)/shard_map/ppermute | solution.py:314
  141.6 5.1 %collective-permute-done.20.refs_5_ = bf16[216,640]{1,0:T(8,128)(2,1)S(1)} collective-permute-done((bf16[216,640]{1,0:T(8,128)(2,1)S(1)}, bf16[216,640]{1,0:T(8,128)(2,1)S(1)}, u32[]{:S(2)}, u32[]{:S(2)}) %collective-permute-start.20) | collective-permute-done | bytes 276512 | tf_op jit(solution)/shard_map/ppermute | solution.py:314
  146.7 7.2 %collective-permute-done.21.refs_6_ = bf16[216,640]{1,0:T(8,128)(2,1)S(1)} collective-permute-done((bf16[216,640]{1,0:T(8,128)(2,1)S(1)}, bf16[216,640]{1,0:T(8,128)(2,1)S(1)}, u32[]{:S(2)}, u32[]{:S(2)}) %collective-permute-start.21) | collective-permute-done | bytes 276512 | tf_op jit(solution)/shard_map/ppermute | solution.py:314
  154.0 5.7 %collective-permute-done.22.refs_7_ = bf16[216,640]{1,0:T(8,128)(2,1)S(1)} collective-permute-done((bf16[216,640]{1,0:T(8,128)(2,1)S(1)}, bf16[216,640]{1,0:T(8,128)(2,1)S(1)}, u32[]{:S(2)}, u32[]{:S(2)}) %collective-permute-start.22) | collective-permute-done | bytes 276512 | tf_op jit(solution)/shard_map/ppermute | solution.py:314
  159.6 2.7 %shard_map.129 = (bf16[216,5120]{1,0:T(8,128)(2,1)}, f32[1,216]{1,0:T(1,128)}) custom-call(bf16[216,640]{1,0:T(8,128)(2,1)S(1)} %get-tuple-element.64.refs_0_, bf16[216,640]{1,0:T(8,128)(2,1)S(1)} %collective-permute-done.16.refs_1_, bf16[216,640]{1,0:T(8,128)(2,1)S(1)} %collective-permute-done.17.refs_2_, ...), custom_call_target="tpu_custom_call" | custom-call | tf_op jit(solution)/shard_map/pallas_call | solution.py:383
  (29 shorter events, 11.2 us)
Async XLA Ops:
  0.6 19.9 %copy-start = (bf16[160,6912]{1,0:T(8,128)(2,1)S(1)}, bf16[160,6912]{1,0:T(8,128)(2,1)}, u32[]{:S(2)}) copy-start(bf16[160,6912]{1,0:T(8,128)(2,1)} %weight.5) | copy-start | bytes 6635524
  2.1 20.4 %collective-permute-start.7 = (bf16[1168,128]{1,0:T(8,128)(2,1)S(1)}, bf16[1168,128]{1,0:T(8,128)(2,1)S(1)}, u32[]{:S(2)}, u32[]{:S(2)}) collective-permute-start(bf16[1168,128]{1,0:T(8,128)(2,1)S(1)} %get-tuple-element.51), channel_id=1, source_target_pairs={{0,32},{2,34},{4,36},{6,38},{8,40},{10,42},{12,44},{14,46},{16,48}... | collective-permute-start | bytes 897032 | tf_op jit(solution)/shard_map/ppermute | solution.py:314
  12.1 22.0 %collective-permute-start = (bf16[1168,128]{1,0:T(8,128)(2,1)S(1)}, bf16[1168,128]{1,0:T(8,128)(2,1)S(1)}, u32[]{:S(2)}, u32[]{:S(2)}) collective-permute-start(bf16[1168,128]{1,0:T(8,128)(2,1)S(1)} %get-tuple-element.43), channel_id=1, source_target_pairs={{0,8},{2,10},{4,12},{6,14},{8,16},{10,18},{12,20},{14,22},{16,24},... | collective-permute-start | bytes 897032 | tf_op jit(solution)/shard_map/ppermute | solution.py:314
  13.2 24.1 %collective-permute-start.1 = (bf16[1168,128]{1,0:T(8,128)(2,1)S(1)}, bf16[1168,128]{1,0:T(8,128)(2,1)S(1)}, u32[]{:S(2)}, u32[]{:S(2)}) collective-permute-start(bf16[1168,128]{1,0:T(8,128)(2,1)S(1)} %get-tuple-element.44), channel_id=1, source_target_pairs={{0,56},{2,58},{4,60},{6,62},{8,0},{10,2},{12,4},{14,6},{16,8},{18,... | collective-permute-start | bytes 897032 | tf_op jit(solution)/shard_map/ppermute | solution.py:314
  15.5 31.0 %collective-permute-start.8 = (bf16[1168,128]{1,0:T(8,128)(2,1)S(1)}, bf16[1168,128]{1,0:T(8,128)(2,1)S(1)}, u32[]{:S(2)}, u32[]{:S(2)}) collective-permute-start(bf16[1168,128]{1,0:T(8,128)(2,1)S(1)} %get-tuple-element.52), channel_id=1, source_target_pairs={{0,24},{2,26},{4,28},{6,30},{8,32},{10,34},{12,36},{14,38},{16,40}... | collective-permute-start | bytes 897032 | tf_op jit(solution)/shard_map/ppermute | solution.py:314
  16.2 33.0 %collective-permute-start.9 = (bf16[1168,128]{1,0:T(8,128)(2,1)S(1)}, bf16[1168,128]{1,0:T(8,128)(2,1)S(1)}, u32[]{:S(2)}, u32[]{:S(2)}) collective-permute-start(bf16[1168,128]{1,0:T(8,128)(2,1)S(1)} %get-tuple-element.53), channel_id=1, source_target_pairs={{0,40},{2,42},{4,44},{6,46},{8,48},{10,50},{12,52},{14,54},{16,56}... | collective-permute-start | bytes 897032 | tf_op jit(solution)/shard_map/ppermute | solution.py:314
  22.5 55.7 %collective-permute-start.13 = (bf16[8,320,128]{2,1,0:T(8,128)(2,1)S(1)}, bf16[8,320,128]{2,1,0:T(8,128)(2,1)S(1)}, u32[]{:S(2)}, u32[]{:S(2)}) collective-permute-start(bf16[8,320,128]{2,1,0:T(8,128)(2,1)S(1)} %get-tuple-element.61), channel_id=1, source_target_pairs={{0,2},{2,0},{4,6},{6,4},{8,10},{10,8},{12,14},{14,12},{16,18},{18,... | collective-permute-start | bytes 1966088 | tf_op jit(solution)/shard_map/ppermute | solution.py:319
  34.2 46.3 %collective-permute-start.14 = (bf16[8,320,128]{2,1,0:T(8,128)(2,1)S(1)}, bf16[8,320,128]{2,1,0:T(8,128)(2,1)S(1)}, u32[]{:S(2)}, u32[]{:S(2)}) collective-permute-start(bf16[8,320,128]{2,1,0:T(8,128)(2,1)S(1)} %get-tuple-element.62), channel_id=1, source_target_pairs={{0,4},{2,6},{4,0},{6,2},{8,12},{10,14},{12,8},{14,10},{16,20},{18,... | collective-permute-start | bytes 1966088 | tf_op jit(solution)/shard_map/ppermute | solution.py:319
  37.4 43.4 %collective-permute-start.15 = (bf16[8,320,128]{2,1,0:T(8,128)(2,1)S(1)}, bf16[8,320,128]{2,1,0:T(8,128)(2,1)S(1)}, u32[]{:S(2)}, u32[]{:S(2)}) collective-permute-start(bf16[8,320,128]{2,1,0:T(8,128)(2,1)S(1)} %get-tuple-element.63), channel_id=1, source_target_pairs={{0,6},{2,4},{4,2},{6,0},{8,14},{10,12},{12,10},{14,8},{16,22},{18,... | collective-permute-start | bytes 1966088 | tf_op jit(solution)/shard_map/ppermute | solution.py:319
  46.4 16.4 %collective-permute-start.2 = (bf16[1168,128]{1,0:T(8,128)(2,1)S(1)}, bf16[1168,128]{1,0:T(8,128)(2,1)S(1)}, u32[]{:S(2)}, u32[]{:S(2)}) collective-permute-start(bf16[1168,128]{1,0:T(8,128)(2,1)S(1)} %get-tuple-element.45), channel_id=1, source_target_pairs={{0,16},{2,18},{4,20},{6,22},{8,24},{10,26},{12,28},{14,30},{16,32}... | collective-permute-start | bytes 897032 | tf_op jit(solution)/shard_map/ppermute | solution.py:314
  49.2 15.5 %collective-permute-start.3 = (bf16[1168,128]{1,0:T(8,128)(2,1)S(1)}, bf16[1168,128]{1,0:T(8,128)(2,1)S(1)}, u32[]{:S(2)}, u32[]{:S(2)}) collective-permute-start(bf16[1168,128]{1,0:T(8,128)(2,1)S(1)} %get-tuple-element.46), channel_id=1, source_target_pairs={{0,48},{2,50},{4,52},{6,54},{8,56},{10,58},{12,60},{14,62},{16,0},... | collective-permute-start | bytes 897032 | tf_op jit(solution)/shard_map/ppermute | solution.py:314
  62.8 10.1 %collective-permute-start.10 = (bf16[3,368,128]{2,1,0:T(8,128)(2,1)S(1)}, bf16[3,368,128]{2,1,0:T(8,128)(2,1)S(1)}, u32[]{:S(2)}, u32[]{:S(2)}) collective-permute-start(bf16[3,368,128]{2,1,0:T(8,128)(2,1)S(1)} %get-tuple-element.55), channel_id=1, source_target_pairs={{0,2},{2,0},{4,6},{6,4},{8,10},{10,8},{12,14},{14,12},{16,18},{18,... | collective-permute-start | bytes 847880 | tf_op jit(solution)/shard_map/ppermute | solution.py:319
  64.7 21.4 %collective-permute-start.11 = (bf16[3,368,128]{2,1,0:T(8,128)(2,1)S(1)}, bf16[3,368,128]{2,1,0:T(8,128)(2,1)S(1)}, u32[]{:S(2)}, u32[]{:S(2)}) collective-permute-start(bf16[3,368,128]{2,1,0:T(8,128)(2,1)S(1)} %get-tuple-element.56), channel_id=1, source_target_pairs={{0,4},{2,6},{4,0},{6,2},{8,12},{10,14},{12,8},{14,10},{16,20},{18,... | collective-permute-start | bytes 847880 | tf_op jit(solution)/shard_map/ppermute | solution.py:319
  73.0 16.8 %collective-permute-start.12 = (bf16[3,368,128]{2,1,0:T(8,128)(2,1)S(1)}, bf16[3,368,128]{2,1,0:T(8,128)(2,1)S(1)}, u32[]{:S(2)}, u32[]{:S(2)}) collective-permute-start(bf16[3,368,128]{2,1,0:T(8,128)(2,1)S(1)} %get-tuple-element.57), channel_id=1, source_target_pairs={{0,6},{2,4},{4,2},{6,0},{8,14},{10,12},{12,10},{14,8},{16,22},{18,... | collective-permute-start | bytes 847880 | tf_op jit(solution)/shard_map/ppermute | solution.py:319
  78.2 18.6 %collective-permute-start.4 = (bf16[5,368,128]{2,1,0:T(8,128)(2,1)S(1)}, bf16[5,368,128]{2,1,0:T(8,128)(2,1)S(1)}, u32[]{:S(2)}, u32[]{:S(2)}) collective-permute-start(bf16[5,368,128]{2,1,0:T(8,128)(2,1)S(1)} %get-tuple-element.48), channel_id=1, source_target_pairs={{0,2},{2,0},{4,6},{6,4},{8,10},{10,8},{12,14},{14,12},{16,18},{18,... | collective-permute-start | bytes 1413128 | tf_op jit(solution)/shard_map/ppermute | solution.py:319
  80.4 24.6 %collective-permute-start.5 = (bf16[5,368,128]{2,1,0:T(8,128)(2,1)S(1)}, bf16[5,368,128]{2,1,0:T(8,128)(2,1)S(1)}, u32[]{:S(2)}, u32[]{:S(2)}) collective-permute-start(bf16[5,368,128]{2,1,0:T(8,128)(2,1)S(1)} %get-tuple-element.49), channel_id=1, source_target_pairs={{0,4},{2,6},{4,0},{6,2},{8,12},{10,14},{12,8},{14,10},{16,20},{18,... | collective-permute-start | bytes 1413128 | tf_op jit(solution)/shard_map/ppermute | solution.py:319
  80.8 24.2 %collective-permute-start.6 = (bf16[5,368,128]{2,1,0:T(8,128)(2,1)S(1)}, bf16[5,368,128]{2,1,0:T(8,128)(2,1)S(1)}, u32[]{:S(2)}, u32[]{:S(2)}) collective-permute-start(bf16[5,368,128]{2,1,0:T(8,128)(2,1)S(1)} %get-tuple-element.50), channel_id=1, source_target_pairs={{0,6},{2,4},{4,2},{6,0},{8,14},{10,12},{12,10},{14,8},{16,22},{18,... | collective-permute-start | bytes 1413128 | tf_op jit(solution)/shard_map/ppermute | solution.py:319
  86.0 32.2 %collective-permute-start.16 = (bf16[216,640]{1,0:T(8,128)(2,1)S(1)}, bf16[216,640]{1,0:T(8,128)(2,1)S(1)}, u32[]{:S(2)}, u32[]{:S(2)}) collective-permute-start(bf16[216,640]{1,0:T(8,128)(2,1)S(1)} %get-tuple-element.65), channel_id=1, source_target_pairs={{0,8},{2,10},{4,12},{6,14},{8,16},{10,18},{12,20},{14,22},{16,24},... | collective-permute-start | bytes 829448 | tf_op jit(solution)/shard_map/ppermute | solution.py:314
  89.8 28.5 %collective-permute-start.17 = (bf16[216,640]{1,0:T(8,128)(2,1)S(1)}, bf16[216,640]{1,0:T(8,128)(2,1)S(1)}, u32[]{:S(2)}, u32[]{:S(2)}) collective-permute-start(bf16[216,640]{1,0:T(8,128)(2,1)S(1)} %get-tuple-element.66), channel_id=1, source_target_pairs={{0,16},{2,18},{4,20},{6,22},{8,24},{10,26},{12,28},{14,30},{16,32}... | collective-permute-start | bytes 829448 | tf_op jit(solution)/shard_map/ppermute | solution.py:314
  105.0 8.2 %collective-permute-start.23 = (f32[32,128]{1,0:T(8,128)S(1)}, f32[32,128]{1,0:T(8,128)S(1)}, u32[]{:S(2)}, u32[]{:S(2)}) collective-permute-start(f32[32,128]{1,0:T(8,128)S(1)} %shard_map.127.mine), channel_id=1, source_target_pairs={{0,1},{1,0},{2,3},{3,2},{4,5},{5,4},{6,7},{7,6},{8,9},{9,8},{10,11... | collective-permute-start | bytes 49160 | tf_op jit(solution)/shard_map/ppermute | solution.py:381
  106.0 19.2 %collective-permute-start.18 = (bf16[216,640]{1,0:T(8,128)(2,1)S(1)}, bf16[216,640]{1,0:T(8,128)(2,1)S(1)}, u32[]{:S(2)}, u32[]{:S(2)}) collective-permute-start(bf16[216,640]{1,0:T(8,128)(2,1)S(1)} %get-tuple-element.67), channel_id=1, source_target_pairs={{0,24},{2,26},{4,28},{6,30},{8,32},{10,34},{12,36},{14,38},{16,40}... | collective-permute-start | bytes 829448 | tf_op jit(solution)/shard_map/ppermute | solution.py:314
  107.2 34.5 %collective-permute-start.19 = (bf16[216,640]{1,0:T(8,128)(2,1)S(1)}, bf16[216,640]{1,0:T(8,128)(2,1)S(1)}, u32[]{:S(2)}, u32[]{:S(2)}) collective-permute-start(bf16[216,640]{1,0:T(8,128)(2,1)S(1)} %get-tuple-element.68), channel_id=1, source_target_pairs={{0,32},{2,34},{4,36},{6,38},{8,40},{10,42},{12,44},{14,46},{16,48}... | collective-permute-start | bytes 829448 | tf_op jit(solution)/shard_map/ppermute | solution.py:314
  113.3 33.5 %collective-permute-start.20 = (bf16[216,640]{1,0:T(8,128)(2,1)S(1)}, bf16[216,640]{1,0:T(8,128)(2,1)S(1)}, u32[]{:S(2)}, u32[]{:S(2)}) collective-permute-start(bf16[216,640]{1,0:T(8,128)(2,1)S(1)} %get-tuple-element.69), channel_id=1, source_target_pairs={{0,40},{2,42},{4,44},{6,46},{8,48},{10,50},{12,52},{14,54},{16,56}... | collective-permute-start | bytes 829448 | tf_op jit(solution)/shard_map/ppermute | solution.py:314
  118.3 35.7 %collective-permute-start.21 = (bf16[216,640]{1,0:T(8,128)(2,1)S(1)}, bf16[216,640]{1,0:T(8,128)(2,1)S(1)}, u32[]{:S(2)}, u32[]{:S(2)}) collective-permute-start(bf16[216,640]{1,0:T(8,128)(2,1)S(1)} %get-tuple-element.70), channel_id=1, source_target_pairs={{0,48},{2,50},{4,52},{6,54},{8,56},{10,58},{12,60},{14,62},{16,0},... | collective-permute-start | bytes 829448 | tf_op jit(solution)/shard_map/ppermute | solution.py:314
  118.3 41.3 %collective-permute-start.22 = (bf16[216,640]{1,0:T(8,128)(2,1)S(1)}, bf16[216,640]{1,0:T(8,128)(2,1)S(1)}, u32[]{:S(2)}, u32[]{:S(2)}) collective-permute-start(bf16[216,640]{1,0:T(8,128)(2,1)S(1)} %get-tuple-element.71), channel_id=1, source_target_pairs={{0,56},{2,58},{4,60},{6,62},{8,0},{10,2},{12,4},{14,6},{16,8},{18,... | collective-permute-start | bytes 829448 | tf_op jit(solution)/shard_map/ppermute | solution.py:314

commit v4 on v3

--- a/solution.py
+++ b/solution.py
@@ -15,9 +15,8 @@
 RANK = 32
 SPAN = NQ * COLS
 TILES = 7
-EXTRA = 48
-BLOCK = TILES * ROWS + EXTRA
-PART = 2 * ROWS + EXTRA
+BLOCK = TILES * ROWS + 8
+PART = 2 * ROWS + 16
 LAST = 51
 
 FIRST = (4,)
@@ -36,14 +35,6 @@
 
 def rows(shape):
     return lax.broadcasted_iota(jnp.int32, shape, len(shape) - 2)
-
-
-def place_t(low_t, period, first):
-    shape = (RANK, 128)
-    hit = (lanes(shape) >= first) & ((lanes(shape) - first) % period == rows(shape))
-    return lax.dot_general(
-        low_t, hit.astype(bf16), (((0,), (0,)), ((), ())), preferred_element_type=f32
-    )
 
 
 def window_of(shift):
@@ -86,27 +77,28 @@
         copy.start()
     for copy in others:
         copy.wait()
-    low_g = place_t(lows[0], 128, 96)
-    low_u = place_t(lows[1], 32, 0)
-    group = lanes((40, 128)) // 32
-    packed = jnp.zeros((40, 128), f32)
-    for g in range(4):
-        packed = jnp.where(group == g, low_u[40 * g : 40 * g + 40], packed)
+    mine = jnp.where(lax.axis_index("cols") == 0, lows[0].astype(f32), lows[1].astype(f32))
+    shape = (RANK, 128)
+    low = lax.dot_general(
+        mine.astype(bf16),
+        (lanes(shape) == rows(shape) + 96).astype(bf16),
+        (((0,), (0,)), ((), ())),
+        preferred_element_type=f32,
+    )
     norm = jnp.concatenate([norms[0] + norms[1], jnp.zeros((1, 48), f32)], axis=1)
-    norm = jnp.broadcast_to(norm, (8, 128))
-    extra = jnp.concatenate([packed, norm], axis=0).astype(bf16)
-    tail[0:ROWS, :] = low_g.astype(bf16)
-    tail[ROWS : ROWS + EXTRA, :] = extra
+    extra = jnp.broadcast_to(norm, (8, 128))
+    tail[0:ROWS, :] = low
+    tail[ROWS : ROWS + 8, :] = extra
     copies[0].wait()
-    pack_block(windows[0], FIRST[0], low_g, extra, out)
+    pack_block(windows[0], FIRST[0], low, extra.astype(bf16), out)
 
 
 def pack_rest(weight, tail, *refs):
     shifts = (*EARLY, *LATE, 0)
     outs, windows, sem = refs[: len(shifts)], refs[-2], refs[-1]
     copies = fetch(weight, windows, sem, shifts)
-    low = tail[0:ROWS, :].astype(f32)
-    extra = tail[ROWS : ROWS + EXTRA, :]
+    low = tail[0:ROWS, :]
+    extra = tail[ROWS : ROWS + 8, :].astype(bf16)
     for i, k in enumerate(shifts):
         copies[i].wait()
         pack_block(windows[i], k, low, extra, outs[i])
@@ -128,7 +120,8 @@
             parts[p][z, ROWS : 2 * ROWS, :] = x[:, 128:].astype(bf16)
 
 
-def turn_high(high_gate, high_up, mix, high, highs, sem):
+def turn_high(high_gate, high_up, *refs):
+    turned, highs, sem = refs[:2], refs[2], refs[3]
     start = COLS * lax.axis_index("zero")
     tile = jnp.minimum(start // 128, LAST)
     own = pl.ds(pl.multiple_of(tile * 128, 128), 384)
@@ -140,19 +133,13 @@
         copy.start()
     for copy in copies:
         copy.wait()
-
-    def own_high(i):
+    shape = (RANK, 128)
+    half = jnp.where(lanes(shape) == rows(shape), MIX, 0.0).astype(bf16)
+    for i in range(2):
         x = pltpu.roll(highs[i].astype(f32), (384 - (start - 128 * tile)) % 384, 1)
-        return x[:, :256].astype(bf16)
-
-    def turned(h, first, width):
-        shape = (RANK, width)
-        hit = jnp.where(lanes(shape) == rows(shape) + first, MIX, 0.0).astype(bf16)
-        return lax.dot_general(h, hit, (((0,), (0,)), ((), ())), preferred_element_type=f32)
-
-    eye = (lanes((256, 256)) == rows((256, 256))) & (rows((256, 256)) < COLS)
-    mix[...] = (eye.astype(f32) + turned(own_high(0), COLS, 256)).astype(bf16)
-    high[...] = turned(own_high(1), 0, 128).astype(bf16)
+        turned[i][...] = lax.dot_general(
+            x[:, :256].astype(bf16), half, (((0,), (0,)), ((), ())), preferred_element_type=f32
+        ).astype(bf16)
 
 
 def turn_up(*refs):
@@ -178,6 +165,8 @@
     wide = (ROWS, 128)
     for i, block in enumerate(blocks):
         low = pltpu.roll(block[ROWS * 6 : ROWS * 7, :].astype(f32), 120, 1)
+        norm = block[ROWS * TILES : BLOCK, :].astype(f32)
+        norm = jnp.concatenate([norm, norm], axis=0).astype(bf16)
         for p in range(NQ):
             start = COLS * jnp.bitwise_xor(q, p)
             tile = jnp.minimum(start // 128, TILES - 3)
@@ -192,7 +181,7 @@
             last = jnp.where(lanes(wide) < 88, x[:, 128:], jnp.where(lanes(wide) < 120, low, 0.0))
             parts[p][i, 0:ROWS, :] = x[:, :128].astype(bf16)
             parts[p][i, ROWS : 2 * ROWS, :] = last.astype(bf16)
-            parts[p][i, 2 * ROWS : PART, :] = block[ROWS * TILES : BLOCK, :]
+            parts[p][i, 2 * ROWS : PART, :] = norm
 
 
 def scales(total):
@@ -215,7 +204,7 @@
         half, j = (0, i) if i < len(NEAR) else (1, i - len(NEAR))
         for p in range(NQ):
             extra = refs[NQ * half + p][j, 2 * ROWS : PART, :].astype(f32)
-            refs[2 * NQ][pl.ds(NQ * z + jnp.bitwise_xor(q, p), 1), :] = extra[40:41]
+            refs[2 * NQ][pl.ds(NQ * z + jnp.bitwise_xor(q, p), 1), :] = extra[0:1]
 
 
 def norm_join(mine, other, out):
@@ -239,33 +228,50 @@
     out[...] = total.astype(bf16)
 
 
-def last_gate(*refs):
-    near, far, (mix, out, scale, low) = refs[:NQ], refs[NQ : 2 * NQ], refs[2 * NQ : 2 * NQ + 4]
-    x, lows, sums = refs[2 * NQ + 4 :]
+def block_of(i, halves):
+    return (halves[:NQ], i) if i < len(NEAR) else (halves[NQ:], i - len(NEAR))
+
+
+def low_rows(*refs):
+    halves, out, x = refs[: 2 * NQ], refs[2 * NQ], refs[2 * NQ + 1]
     place = lax.axis_index("zero")
     q, here = place % NQ, place // NQ
+    pick = (lanes((RANK, 128)) == rows((RANK, 128)) + (COLS - 128)).astype(bf16)
+    for i, k in enumerate(ORDER):
+        parts, j = block_of(i, halves)
+        for p in range(NQ):
+            at = pl.multiple_of(jnp.bitwise_xor(q, p) * ROWS, ROWS)
+            x[i % 2, pl.ds(at, ROWS), :] = parts[p][j, ROWS : 2 * ROWS, :]
+        at = pl.multiple_of((here + NZ - k) % NZ * 640, 640)
+        out[:, pl.ds(at, 640)] = lax.dot_general(
+            pick, x[i % 2], (((1,), (1,)), ((), ())), preferred_element_type=f32
+        ).astype(bf16)
+
+
+def last_gate(*refs):
+    halves, (high, mine, other, out, scale, low_up) = refs[: 2 * NQ], refs[2 * NQ : 2 * NQ + 6]
+    x, sums = refs[2 * NQ + 6 :]
+    place = lax.axis_index("zero")
+    q, here = place % NQ, place // NQ
+    has_gate = lax.axis_index("cols") == 0
     total = jnp.zeros((COLS, 128), f32)
-    m = mix[0:COLS, :]
-    pick = (lanes((RANK, 128)) == rows((RANK, 128))).astype(bf16)
-    turned = (((1,), (1,)), ((), ()))
+    eye = (lanes((COLS, 256)) == rows((COLS, 256))).astype(bf16)
+    h = high[0:COLS, 0:RANK]
     for i, k in enumerate(ORDER):
-        parts, j = (near, i) if i < len(NEAR) else (far, i - len(NEAR))
+        parts, j = block_of(i, halves)
         for p in range(NQ):
             at = pl.multiple_of(jnp.bitwise_xor(q, p) * ROWS, ROWS)
             x[i % 2, pl.ds(at, ROWS), 0:128] = parts[p][j, 0:ROWS, :]
             x[i % 2, pl.ds(at, ROWS), 128:256] = parts[p][j, ROWS : 2 * ROWS, :]
-            extra = parts[p][j, 2 * ROWS : PART, :].astype(f32)[0:40]
-            wide = jnp.concatenate(
-                [pltpu.roll(extra, (128 - 32 * g) % 128, 1) for g in range(4)], axis=0
-            )
-            lows[i % 2, pl.ds(at, ROWS), :] = wide.astype(bf16)
         at = pl.multiple_of((here + NZ - k) % NZ * 640, 640)
-        r = lax.dot_general(m, x[i % 2], turned, preferred_element_type=f32)
+        a, b = mine[:, pl.ds(at, 640)].astype(f32), other[:, pl.ds(at, 640)].astype(f32)
+        low = jnp.where(has_gate, a, b).astype(bf16)
+        low_up[:, pl.ds(at, 640)] = jnp.where(has_gate, b, a).astype(bf16)
+        r = lax.dot_general(
+            eye, x[i % 2], (((1,), (1,)), ((), ())), preferred_element_type=f32
+        ) + jnp.dot(h, low, preferred_element_type=f32)
         sums[:, pl.ds(at, 640)] = r
         total = total + magnitudes(r)
-        low[:, pl.ds(at, 640)] = lax.dot_general(
-            pick, lows[i % 2], turned, preferred_element_type=f32
-        ).astype(bf16)
     column, row = scales(total)
     scale[...] = row
     out[...] = (sums[...] * (1.0 / column)).astype(bf16)
@@ -328,7 +334,7 @@
     inward = {}
     first, tail = kernel(
         pack_first,
-        [((BLOCK, 128), bf16), ((ROWS + EXTRA, 128), bf16)],
+        [((BLOCK, 128), bf16), ((ROWS + 8, 128), f32)],
         [
             pltpu.VMEM((1, ROWS, 1024), bf16),
             pltpu.VMEM((2, RANK, ROWS), bf16),
@@ -362,30 +368,31 @@
             split_gate, [((len(shifts), PART, 128), bf16)] * NQ
         )(*[inward[k] for k in shifts])
         halves.append(across(parts))
-    mix, high = kernel(
+    arrived = (*halves[0], *halves[1])
+    (norm,) = kernel(norm_rows, [((NZ * NQ, 128), f32)])(*arrived)
+    (low,) = kernel(
+        low_rows, [((RANK, D_MODEL), bf16)], [pltpu.VMEM((2, NQ * ROWS, 128), bf16)]
+    )(*arrived)
+    other_low = lax.ppermute(low, "cols", [(0, 1), (1, 0)])
+    other = lax.ppermute(norm, "cols", [(0, 1), (1, 0)])
+    high_g, high_u = kernel(
         turn_high,
-        [((256, 256), bf16), ((256, 128), bf16)],
+        [((256, 128), bf16)] * 2,
         [pltpu.VMEM((2, RANK, 384), bf16), dma((2,))],
         [HBM, HBM],
     )(hbm(high_gate), hbm(high_up))
-    (norm,) = kernel(norm_rows, [((NZ * NQ, 128), f32)])(*halves[0], *halves[1])
-    final_gate, scale_gate, low = kernel(
+    (serve_norm,) = kernel(norm_join, [((40, 128), bf16)])(norm, other)
+    final_gate, scale_gate, low_u = kernel(
         last_gate,
         [((COLS, D_MODEL), bf16), ((1, COLS), f32), ((RANK, D_MODEL), bf16)],
-        [
-            pltpu.VMEM((2, NQ * ROWS, 256), bf16),
-            pltpu.VMEM((2, NQ * ROWS, 128), bf16),
-            pltpu.VMEM((COLS, D_MODEL), f32),
-        ],
-    )(*halves[0], *halves[1], mix)
-    other = lax.ppermute(norm, "cols", [(0, 1), (1, 0)])
-    (serve_norm,) = kernel(norm_join, [((40, 128), bf16)])(norm, other)
+        [pltpu.VMEM((2, NQ * ROWS, 256), bf16), pltpu.VMEM((COLS, D_MODEL), f32)],
+    )(*arrived, high_g, low, other_low)
     final_up, scale_up = kernel(
         last_up,
         [((COLS, D_MODEL), bf16), ((1, COLS), f32)],
         [pltpu.VMEM((COLS, D_MODEL), f32)],
         [VMEM] * (NZ + 2) + [HBM],
-    )(*up_in, high, low, hbm(serve_norm))
+    )(*up_in, high_u, low_u, hbm(serve_norm))
     return (final_gate.T, final_up.T, scale_gate[0], scale_up[0], serve_norm.reshape(D_MODEL))
 
 

time: 163 us -> 191 us (1.17)
  waiting for transfers between devices: 84.2 us -> 102 us
  starting transfers between devices: 59.4 us -> 67.1 us
    ppermute x9, waiting for transfers between devices: 20.3 us -> 45.9 us  [across(): lax.ppermute(part, 'zero', [(s, s ^ p) for s in range(NZ * NQ)])]
    ppermute x14, waiting for transfers between devices: 63.9 us -> 56.6 us  [along_z(): return lax.ppermute(block, 'zero', pairs)]
    ppermute x14, starting transfers between devices: 37.5 us -> 43.1 us  [along_z(): return lax.ppermute(block, 'zero', pairs)]
  transfers between devices with their start and end apart: 24 -> 25, of which waited for: 13 -> 13; matrix products, arithmetic and copies ran while one was open for 0% -> 0% of each run, Pallas kernels for 9% -> 8%
where the time goes in v4:
time: 191 us; the launch traced here: 189 us
  waiting for transfers between devices  102 us (53%)
  starting transfers between devices  67.1 us (35%)
  Pallas kernels  18.4 us (10%)
    ppermute x14, waiting for transfers between devices, along_z(): return lax.ppermute(block, 'zero', pairs)  56.6 us
    ppermute x9, waiting for transfers between devices, across(): lax.ppermute(part, 'zero', [(s, s ^ p) for s in range(NZ * NQ)])  45.9 us
    ppermute x14, starting transfers between devices, along_z(): return lax.ppermute(block, 'zero', pairs)  43.1 us
    ppermute x9, starting transfers between devices, across(): lax.ppermute(part, 'zero', [(s, s ^ p) for s in range(NZ * NQ)])  21.9 us
  transfers between devices with their start and end apart: 25, of which 13 were waited for; matrix products, arithmetic and copies ran while one was open for 0% of the time, Pallas kernels for 8%

profile of v4, /device:TPU:6, one launch (start us, length us, event | category | flops | bytes accessed | tf_op | source)
XLA Modules:
  0.0 188.8 jit_solution(5818336168742799992)
XLA Ops:
  2.0 7.3 %collective-permute-start.7 = (bf16[1128,128]{1,0:T(8,128)(2,1)S(1)}, bf16[1128,128]{1,0:T(8,128)(2,1)S(1)}, u32[]{:S(2)}, u32[]{:S(2)}) collective-permute-start(bf16[1128,128]{1,0:T(8,128)(2,1)S(1)} %get-tuple-element.51), channel_id=1, source_target_pairs={{0,32},{2,34},{4,36},{6,38},{8,40},{10,42},{12,44},{14,46},{16,48}... | collective-permute-start | bytes 866312 | tf_op jit(solution)/shard_map/ppermute | solution.py:320
  9.2 2.9 %shard_map.120 = (bf16[1128,128]{1,0:T(8,128)(2,1)S(1)}, bf16[1128,128]{1,0:T(8,128)(2,1)S(1)}, bf16[1128,128]{1,0:T(8,128)(2,1)S(1)}, bf16[1128,128]{1,0:T(8,12...) custom-call(bf16[160,6912]{1,0:T(8,128)(2,1)} %weight.4, ...), custom_call_target="tpu_custom_call" | custom-call | tf_op jit(solution)/shard_map/pallas_call | solution.py:349
  12.1 2.0 %collective-permute-start.8 = (bf16[1128,128]{1,0:T(8,128)(2,1)S(1)}, bf16[1128,128]{1,0:T(8,128)(2,1)S(1)}, u32[]{:S(2)}, u32[]{:S(2)}) collective-permute-start(bf16[1128,128]{1,0:T(8,128)(2,1)S(1)} %get-tuple-element.52), channel_id=1, source_target_pairs={{0,24},{2,26},{4,28},{6,30},{8,32},{10,34},{12,36},{14,38},{16,40}... | collective-permute-start | bytes 866312 | tf_op jit(solution)/shard_map/ppermute | solution.py:320
  14.1 3.1 %collective-permute-start.9 = (bf16[1128,128]{1,0:T(8,128)(2,1)S(1)}, bf16[1128,128]{1,0:T(8,128)(2,1)S(1)}, u32[]{:S(2)}, u32[]{:S(2)}) collective-permute-start(bf16[1128,128]{1,0:T(8,128)(2,1)S(1)} %get-tuple-element.53), channel_id=1, source_target_pairs={{0,40},{2,42},{4,44},{6,46},{8,48},{10,50},{12,52},{14,54},{16,56}... | collective-permute-start | bytes 866312 | tf_op jit(solution)/shard_map/ppermute | solution.py:320
  18.3 2.2 %collective-permute-start.1 = (bf16[1128,128]{1,0:T(8,128)(2,1)S(1)}, bf16[1128,128]{1,0:T(8,128)(2,1)S(1)}, u32[]{:S(2)}, u32[]{:S(2)}) collective-permute-start(bf16[1128,128]{1,0:T(8,128)(2,1)S(1)} %get-tuple-element.44), channel_id=1, source_target_pairs={{0,56},{2,58},{4,60},{6,62},{8,0},{10,2},{12,4},{14,6},{16,8},{18,... | collective-permute-start | bytes 866312 | tf_op jit(solution)/shard_map/ppermute | solution.py:320
  20.5 6.3 %collective-permute-done.7.refs_0_ = bf16[1128,128]{1,0:T(8,128)(2,1)S(1)} collective-permute-done((bf16[1128,128]{1,0:T(8,128)(2,1)S(1)}, bf16[1128,128]{1,0:T(8,128)(2,1)S(1)}, u32[]{:S(2)}, u32[]{:S(2)}) %collective-permute-start.7) | collective-permute-done | bytes 288800 | tf_op jit(solution)/shard_map/ppermute | solution.py:320
  26.8 2.0 %collective-permute-start.2 = (bf16[1128,128]{1,0:T(8,128)(2,1)S(1)}, bf16[1128,128]{1,0:T(8,128)(2,1)S(1)}, u32[]{:S(2)}, u32[]{:S(2)}) collective-permute-start(bf16[1128,128]{1,0:T(8,128)(2,1)S(1)} %get-tuple-element.45), channel_id=1, source_target_pairs={{0,16},{2,18},{4,20},{6,22},{8,24},{10,26},{12,28},{14,30},{16,32}... | collective-permute-start | bytes 866312 | tf_op jit(solution)/shard_map/ppermute | solution.py:320
  28.8 11.7 %collective-permute-done.8.refs_1_ = bf16[1128,128]{1,0:T(8,128)(2,1)S(1)} collective-permute-done((bf16[1128,128]{1,0:T(8,128)(2,1)S(1)}, bf16[1128,128]{1,0:T(8,128)(2,1)S(1)}, u32[]{:S(2)}, u32[]{:S(2)}) %collective-permute-start.8) | collective-permute-done | bytes 288800 | tf_op jit(solution)/shard_map/ppermute | solution.py:320
  40.5 4.8 %collective-permute-start.3 = (bf16[1128,128]{1,0:T(8,128)(2,1)S(1)}, bf16[1128,128]{1,0:T(8,128)(2,1)S(1)}, u32[]{:S(2)}, u32[]{:S(2)}) collective-permute-start(bf16[1128,128]{1,0:T(8,128)(2,1)S(1)} %get-tuple-element.46), channel_id=1, source_target_pairs={{0,48},{2,50},{4,52},{6,54},{8,56},{10,58},{12,60},{14,62},{16,0},... | collective-permute-start | bytes 866312 | tf_op jit(solution)/shard_map/ppermute | solution.py:320
  47.5 5.8 %collective-permute-done.refs_1_ = bf16[1128,128]{1,0:T(8,128)(2,1)S(1)} collective-permute-done((bf16[1128,128]{1,0:T(8,128)(2,1)S(1)}, bf16[1128,128]{1,0:T(8,128)(2,1)S(1)}, u32[]{:S(2)}, u32[]{:S(2)}) %collective-permute-start) | collective-permute-done | bytes 288800 | tf_op jit(solution)/shard_map/ppermute | solution.py:320
  53.3 3.2 %collective-permute-start.11 = (bf16[3,336,128]{2,1,0:T(8,128)(2,1)S(1)}, bf16[3,336,128]{2,1,0:T(8,128)(2,1)S(1)}, u32[]{:S(2)}, u32[]{:S(2)}) collective-permute-start(bf16[3,336,128]{2,1,0:T(8,128)(2,1)S(1)} %get-tuple-element.56), channel_id=1, source_target_pairs={{0,4},{2,6},{4,0},{6,2},{8,12},{10,14},{12,8},{14,10},{16,20},{18,... | collective-permute-start | bytes 774152 | tf_op jit(solution)/shard_map/ppermute | solution.py:325
  56.5 1.7 collective-permute-done.2.refs_3_
  58.2 1.7 collective-permute-done.3.refs_4_
  62.5 4.8 %collective-permute-start.12 = (bf16[3,336,128]{2,1,0:T(8,128)(2,1)S(1)}, bf16[3,336,128]{2,1,0:T(8,128)(2,1)S(1)}, u32[]{:S(2)}, u32[]{:S(2)}) collective-permute-start(bf16[3,336,128]{2,1,0:T(8,128)(2,1)S(1)} %get-tuple-element.57), channel_id=1, source_target_pairs={{0,6},{2,4},{4,2},{6,0},{8,14},{10,12},{12,10},{14,8},{16,22},{18,... | collective-permute-start | bytes 774152 | tf_op jit(solution)/shard_map/ppermute | solution.py:325
  67.3 1.7 shard_map.126
  70.8 4.8 %collective-permute-start.16 = (bf16[8,320,128]{2,1,0:T(8,128)(2,1)S(1)}, bf16[8,320,128]{2,1,0:T(8,128)(2,1)S(1)}, u32[]{:S(2)}, u32[]{:S(2)}) collective-permute-start(bf16[8,320,128]{2,1,0:T(8,128)(2,1)S(1)} %get-tuple-element.63), channel_id=1, source_target_pairs={{0,6},{2,4},{4,2},{6,0},{8,14},{10,12},{12,10},{14,8},{16,22},{18,... | collective-permute-start | bytes 1966088 | tf_op jit(solution)/shard_map/ppermute | solution.py:325
  75.6 8.1 %collective-permute-done.12.refs_7_ = bf16[3,336,128]{2,1,0:T(8,128)(2,1)S(1)} collective-permute-done((bf16[3,336,128]{2,1,0:T(8,128)(2,1)S(1)}, bf16[3,336,128]{2,1,0:T(8,128)(2,1)S(1)}, u32[]{:S(2)}, u32[]{:S(2)}) %collective-permute-start.12) | collective-permute-done | bytes 258080 | tf_op jit(solution)/shard_map/ppermute | solution.py:325
  84.0 4.0 %collective-permute-start.6 = (bf16[5,336,128]{2,1,0:T(8,128)(2,1)S(1)}, bf16[5,336,128]{2,1,0:T(8,128)(2,1)S(1)}, u32[]{:S(2)}, u32[]{:S(2)}) collective-permute-start(bf16[5,336,128]{2,1,0:T(8,128)(2,1)S(1)} %get-tuple-element.50), channel_id=1, source_target_pairs={{0,6},{2,4},{4,2},{6,0},{8,14},{10,12},{12,10},{14,8},{16,22},{18,... | collective-permute-start | bytes 1290248 | tf_op jit(solution)/shard_map/ppermute | solution.py:325
  88.0 37.8 %collective-permute-done.5.refs_2_ = bf16[5,336,128]{2,1,0:T(8,128)(2,1)S(1)} collective-permute-done((bf16[5,336,128]{2,1,0:T(8,128)(2,1)S(1)}, bf16[5,336,128]{2,1,0:T(8,128)(2,1)S(1)}, u32[]{:S(2)}, u32[]{:S(2)}) %collective-permute-start.5) | collective-permute-done | bytes 430112 | tf_op jit(solution)/shard_map/ppermute | solution.py:325
  127.9 2.8 %collective-permute-start.18 = (bf16[216,640]{1,0:T(8,128)(2,1)S(1)}, bf16[216,640]{1,0:T(8,128)(2,1)S(1)}, u32[]{:S(2)}, u32[]{:S(2)}) collective-permute-start(bf16[216,640]{1,0:T(8,128)(2,1)S(1)} %get-tuple-element.66), channel_id=1, source_target_pairs={{0,16},{2,18},{4,20},{6,22},{8,24},{10,26},{12,28},{14,30},{16,32}... | collective-permute-start | bytes 829448 | tf_op jit(solution)/shard_map/ppermute | solution.py:320
  130.7 2.1 %collective-permute-start.24 = (f32[32,128]{1,0:T(8,128)S(1)}, f32[32,128]{1,0:T(8,128)S(1)}, u32[]{:S(2)}, u32[]{:S(2)}) collective-permute-start(f32[32,128]{1,0:T(8,128)S(1)} %shard_map.128.mine), channel_id=1, source_target_pairs={{0,1},{1,0},{2,3},{3,2},{4,5},{5,4},{6,7},{7,6},{8,9},{9,8},{10,11... | collective-permute-start | bytes 49160 | tf_op jit(solution)/shard_map/ppermute | solution.py:377
  132.8 3.6 %collective-permute-start.19 = (bf16[216,640]{1,0:T(8,128)(2,1)S(1)}, bf16[216,640]{1,0:T(8,128)(2,1)S(1)}, u32[]{:S(2)}, u32[]{:S(2)}) collective-permute-start(bf16[216,640]{1,0:T(8,128)(2,1)S(1)} %get-tuple-element.67), channel_id=1, source_target_pairs={{0,24},{2,26},{4,28},{6,30},{8,32},{10,34},{12,36},{14,38},{16,40}... | collective-permute-start | bytes 829448 | tf_op jit(solution)/shard_map/ppermute | solution.py:320
  137.6 3.1 %collective-permute-done.17.refs_1_ = bf16[216,640]{1,0:T(8,128)(2,1)S(1)} collective-permute-done((bf16[216,640]{1,0:T(8,128)(2,1)S(1)}, bf16[216,640]{1,0:T(8,128)(2,1)S(1)}, u32[]{:S(2)}, u32[]{:S(2)}) %collective-permute-start.17) | collective-permute-done | bytes 276512 | tf_op jit(solution)/shard_map/ppermute | solution.py:320
  140.8 5.3 %collective-permute-start.21 = (bf16[216,640]{1,0:T(8,128)(2,1)S(1)}, bf16[216,640]{1,0:T(8,128)(2,1)S(1)}, u32[]{:S(2)}, u32[]{:S(2)}) collective-permute-start(bf16[216,640]{1,0:T(8,128)(2,1)S(1)} %get-tuple-element.69), channel_id=1, source_target_pairs={{0,40},{2,42},{4,44},{6,46},{8,48},{10,50},{12,52},{14,54},{16,56}... | collective-permute-start | bytes 829448 | tf_op jit(solution)/shard_map/ppermute | solution.py:320
  146.0 7.5 %collective-permute-done.18.refs_2_ = bf16[216,640]{1,0:T(8,128)(2,1)S(1)} collective-permute-done((bf16[216,640]{1,0:T(8,128)(2,1)S(1)}, bf16[216,640]{1,0:T(8,128)(2,1)S(1)}, u32[]{:S(2)}, u32[]{:S(2)}) %collective-permute-start.18) | collective-permute-done | bytes 276512 | tf_op jit(solution)/shard_map/ppermute | solution.py:320
  153.5 6.5 %collective-permute-start.22 = (bf16[216,640]{1,0:T(8,128)(2,1)S(1)}, bf16[216,640]{1,0:T(8,128)(2,1)S(1)}, u32[]{:S(2)}, u32[]{:S(2)}) collective-permute-start(bf16[216,640]{1,0:T(8,128)(2,1)S(1)} %get-tuple-element.70), channel_id=1, source_target_pairs={{0,48},{2,50},{4,52},{6,54},{8,56},{10,58},{12,60},{14,62},{16,0},... | collective-permute-start | bytes 829448 | tf_op jit(solution)/shard_map/ppermute | solution.py:320
  163.5 3.7 %shard_map.125 = (bf16[216,5120]{1,0:T(8,128)(2,1)}, f32[1,216]{1,0:T(1,128)}, bf16[32,5120]{1,0:T(8,128)(2,1)S(1)}) custom-call(bf16[5,336,128]{2,1,0:T(8,128)(2,1)S(1)} %get-tuple-element.47.refs_0_, bf16[5,336,128]{2,1,0:T(8,128)(2,1)S(1)} %collective-permute-done.4.refs_1_, bf16[5,336,128]{2,1,0:T(8,128)(2,1)S(1)} %collective-permute-done.5.refs_2_, ...), custom_call_target="tpu_custom_call" | custom-call | tf_op jit(solution)/shard_map/pallas_call | solution.py:385
  167.2 4.4 %collective-permute-done.19.refs_3_ = bf16[216,640]{1,0:T(8,128)(2,1)S(1)} collective-permute-done((bf16[216,640]{1,0:T(8,128)(2,1)S(1)}, bf16[216,640]{1,0:T(8,128)(2,1)S(1)}, u32[]{:S(2)}, u32[]{:S(2)}) %collective-permute-start.19) | collective-permute-done | bytes 276512 | tf_op jit(solution)/shard_map/ppermute | solution.py:320
  171.6 4.8 %collective-permute-done.20.refs_4_ = bf16[216,640]{1,0:T(8,128)(2,1)S(1)} collective-permute-done((bf16[216,640]{1,0:T(8,128)(2,1)S(1)}, bf16[216,640]{1,0:T(8,128)(2,1)S(1)}, u32[]{:S(2)}, u32[]{:S(2)}) %collective-permute-start.20) | collective-permute-done | bytes 276512 | tf_op jit(solution)/shard_map/ppermute | solution.py:320
  176.4 3.3 %collective-permute-done.22.refs_6_ = bf16[216,640]{1,0:T(8,128)(2,1)S(1)} collective-permute-done((bf16[216,640]{1,0:T(8,128)(2,1)S(1)}, bf16[216,640]{1,0:T(8,128)(2,1)S(1)}, u32[]{:S(2)}, u32[]{:S(2)}) %collective-permute-start.22) | collective-permute-done | bytes 276512 | tf_op jit(solution)/shard_map/ppermute | solution.py:320
  179.7 6.3 %collective-permute-done.23.refs_7_ = bf16[216,640]{1,0:T(8,128)(2,1)S(1)} collective-permute-done((bf16[216,640]{1,0:T(8,128)(2,1)S(1)}, bf16[216,640]{1,0:T(8,128)(2,1)S(1)}, u32[]{:S(2)}, u32[]{:S(2)}) %collective-permute-start.23) | collective-permute-done | bytes 276512 | tf_op jit(solution)/shard_map/ppermute | solution.py:320
  186.0 2.7 %shard_map.130 = (bf16[216,5120]{1,0:T(8,128)(2,1)}, f32[1,216]{1,0:T(1,128)}) custom-call(bf16[216,640]{1,0:T(8,128)(2,1)S(1)} %get-tuple-element.64.refs_0_, bf16[216,640]{1,0:T(8,128)(2,1)S(1)} %collective-permute-done.17.refs_1_, bf16[216,640]{1,0:T(8,128)(2,1)S(1)} %collective-permute-done.18.refs_2_, ...), custom_call_target="tpu_custom_call" | custom-call | tf_op jit(solution)/shard_map/pallas_call | solution.py:390
  (32 shorter events, 16.2 us)
Async XLA Ops:
  2.0 24.8 %collective-permute-start.7 = (bf16[1128,128]{1,0:T(8,128)(2,1)S(1)}, bf16[1128,128]{1,0:T(8,128)(2,1)S(1)}, u32[]{:S(2)}, u32[]{:S(2)}) collective-permute-start(bf16[1128,128]{1,0:T(8,128)(2,1)S(1)} %get-tuple-element.51), channel_id=1, source_target_pairs={{0,32},{2,34},{4,36},{6,38},{8,40},{10,42},{12,44},{14,46},{16,48}... | collective-permute-start | bytes 866312 | tf_op jit(solution)/shard_map/ppermute | solution.py:320
  9.2 58.1 %copy-start = (bf16[160,6912]{1,0:T(8,128)(2,1)S(1)}, bf16[160,6912]{1,0:T(8,128)(2,1)}, u32[]{:S(2)}) copy-start(bf16[160,6912]{1,0:T(8,128)(2,1)} %weight.5) | copy-start | bytes 6635524
  12.1 28.4 %collective-permute-start.8 = (bf16[1128,128]{1,0:T(8,128)(2,1)S(1)}, bf16[1128,128]{1,0:T(8,128)(2,1)S(1)}, u32[]{:S(2)}, u32[]{:S(2)}) collective-permute-start(bf16[1128,128]{1,0:T(8,128)(2,1)S(1)} %get-tuple-element.52), channel_id=1, source_target_pairs={{0,24},{2,26},{4,28},{6,30},{8,32},{10,34},{12,36},{14,38},{16,40}... | collective-permute-start | bytes 866312 | tf_op jit(solution)/shard_map/ppermute | solution.py:320
  14.1 31.1 %collective-permute-start.9 = (bf16[1128,128]{1,0:T(8,128)(2,1)S(1)}, bf16[1128,128]{1,0:T(8,128)(2,1)S(1)}, u32[]{:S(2)}, u32[]{:S(2)}) collective-permute-start(bf16[1128,128]{1,0:T(8,128)(2,1)S(1)} %get-tuple-element.53), channel_id=1, source_target_pairs={{0,40},{2,42},{4,44},{6,46},{8,48},{10,50},{12,52},{14,54},{16,56}... | collective-permute-start | bytes 866312 | tf_op jit(solution)/shard_map/ppermute | solution.py:320
  17.3 36.1 %collective-permute-start = (bf16[1128,128]{1,0:T(8,128)(2,1)S(1)}, bf16[1128,128]{1,0:T(8,128)(2,1)S(1)}, u32[]{:S(2)}, u32[]{:S(2)}) collective-permute-start(bf16[1128,128]{1,0:T(8,128)(2,1)S(1)} %get-tuple-element.43), channel_id=1, source_target_pairs={{0,8},{2,10},{4,12},{6,14},{8,16},{10,18},{12,20},{14,22},{16,24},... | collective-permute-start | bytes 866312 | tf_op jit(solution)/shard_map/ppermute | solution.py:320
  18.3 38.2 %collective-permute-start.1 = (bf16[1128,128]{1,0:T(8,128)(2,1)S(1)}, bf16[1128,128]{1,0:T(8,128)(2,1)S(1)}, u32[]{:S(2)}, u32[]{:S(2)}) collective-permute-start(bf16[1128,128]{1,0:T(8,128)(2,1)S(1)} %get-tuple-element.44), channel_id=1, source_target_pairs={{0,56},{2,58},{4,60},{6,62},{8,0},{10,2},{12,4},{14,6},{16,8},{18,... | collective-permute-start | bytes 866312 | tf_op jit(solution)/shard_map/ppermute | solution.py:320
  26.8 31.4 %collective-permute-start.2 = (bf16[1128,128]{1,0:T(8,128)(2,1)S(1)}, bf16[1128,128]{1,0:T(8,128)(2,1)S(1)}, u32[]{:S(2)}, u32[]{:S(2)}) collective-permute-start(bf16[1128,128]{1,0:T(8,128)(2,1)S(1)} %get-tuple-element.45), channel_id=1, source_target_pairs={{0,16},{2,18},{4,20},{6,22},{8,24},{10,26},{12,28},{14,30},{16,32}... | collective-permute-start | bytes 866312 | tf_op jit(solution)/shard_map/ppermute | solution.py:320
  40.5 19.3 %collective-permute-start.3 = (bf16[1128,128]{1,0:T(8,128)(2,1)S(1)}, bf16[1128,128]{1,0:T(8,128)(2,1)S(1)}, u32[]{:S(2)}, u32[]{:S(2)}) collective-permute-start(bf16[1128,128]{1,0:T(8,128)(2,1)S(1)} %get-tuple-element.46), channel_id=1, source_target_pairs={{0,48},{2,50},{4,52},{6,54},{8,56},{10,58},{12,60},{14,62},{16,0},... | collective-permute-start | bytes 866312 | tf_op jit(solution)/shard_map/ppermute | solution.py:320
  46.0 24.4 %collective-permute-start.10 = (bf16[3,336,128]{2,1,0:T(8,128)(2,1)S(1)}, bf16[3,336,128]{2,1,0:T(8,128)(2,1)S(1)}, u32[]{:S(2)}, u32[]{:S(2)}) collective-permute-start(bf16[3,336,128]{2,1,0:T(8,128)(2,1)S(1)} %get-tuple-element.55), channel_id=1, source_target_pairs={{0,2},{2,0},{4,6},{6,4},{8,10},{10,8},{12,14},{14,12},{16,18},{18,... | collective-permute-start | bytes 774152 | tf_op jit(solution)/shard_map/ppermute | solution.py:325
  53.3 17.5 %collective-permute-start.11 = (bf16[3,336,128]{2,1,0:T(8,128)(2,1)S(1)}, bf16[3,336,128]{2,1,0:T(8,128)(2,1)S(1)}, u32[]{:S(2)}, u32[]{:S(2)}) collective-permute-start(bf16[3,336,128]{2,1,0:T(8,128)(2,1)S(1)} %get-tuple-element.56), channel_id=1, source_target_pairs={{0,4},{2,6},{4,0},{6,2},{8,12},{10,14},{12,8},{14,10},{16,20},{18,... | collective-permute-start | bytes 774152 | tf_op jit(solution)/shard_map/ppermute | solution.py:325
  61.1 22.9 %collective-permute-start.4 = (bf16[5,336,128]{2,1,0:T(8,128)(2,1)S(1)}, bf16[5,336,128]{2,1,0:T(8,128)(2,1)S(1)}, u32[]{:S(2)}, u32[]{:S(2)}) collective-permute-start(bf16[5,336,128]{2,1,0:T(8,128)(2,1)S(1)} %get-tuple-element.48), channel_id=1, source_target_pairs={{0,2},{2,0},{4,6},{6,4},{8,10},{10,8},{12,14},{14,12},{16,18},{18,... | collective-permute-start | bytes 1290248 | tf_op jit(solution)/shard_map/ppermute | solution.py:325
  62.5 21.1 %collective-permute-start.12 = (bf16[3,336,128]{2,1,0:T(8,128)(2,1)S(1)}, bf16[3,336,128]{2,1,0:T(8,128)(2,1)S(1)}, u32[]{:S(2)}, u32[]{:S(2)}) collective-permute-start(bf16[3,336,128]{2,1,0:T(8,128)(2,1)S(1)} %get-tuple-element.57), channel_id=1, source_target_pairs={{0,6},{2,4},{4,2},{6,0},{8,14},{10,12},{12,10},{14,8},{16,22},{18,... | collective-permute-start | bytes 774152 | tf_op jit(solution)/shard_map/ppermute | solution.py:325
  69.0 57.5 %collective-permute-start.14 = (bf16[8,320,128]{2,1,0:T(8,128)(2,1)S(1)}, bf16[8,320,128]{2,1,0:T(8,128)(2,1)S(1)}, u32[]{:S(2)}, u32[]{:S(2)}) collective-permute-start(bf16[8,320,128]{2,1,0:T(8,128)(2,1)S(1)} %get-tuple-element.61), channel_id=1, source_target_pairs={{0,2},{2,0},{4,6},{6,4},{8,10},{10,8},{12,14},{14,12},{16,18},{18,... | collective-permute-start | bytes 1966088 | tf_op jit(solution)/shard_map/ppermute | solution.py:325
  70.5 56.0 %collective-permute-start.15 = (bf16[8,320,128]{2,1,0:T(8,128)(2,1)S(1)}, bf16[8,320,128]{2,1,0:T(8,128)(2,1)S(1)}, u32[]{:S(2)}, u32[]{:S(2)}) collective-permute-start(bf16[8,320,128]{2,1,0:T(8,128)(2,1)S(1)} %get-tuple-element.62), channel_id=1, source_target_pairs={{0,4},{2,6},{4,0},{6,2},{8,12},{10,14},{12,8},{14,10},{16,20},{18,... | collective-permute-start | bytes 1966088 | tf_op jit(solution)/shard_map/ppermute | solution.py:325
  70.8 55.7 %collective-permute-start.16 = (bf16[8,320,128]{2,1,0:T(8,128)(2,1)S(1)}, bf16[8,320,128]{2,1,0:T(8,128)(2,1)S(1)}, u32[]{:S(2)}, u32[]{:S(2)}) collective-permute-start(bf16[8,320,128]{2,1,0:T(8,128)(2,1)S(1)} %get-tuple-element.63), channel_id=1, source_target_pairs={{0,6},{2,4},{4,2},{6,0},{8,14},{10,12},{12,10},{14,8},{16,22},{18,... | collective-permute-start | bytes 1966088 | tf_op jit(solution)/shard_map/ppermute | solution.py:325
  83.6 42.2 %collective-permute-start.5 = (bf16[5,336,128]{2,1,0:T(8,128)(2,1)S(1)}, bf16[5,336,128]{2,1,0:T(8,128)(2,1)S(1)}, u32[]{:S(2)}, u32[]{:S(2)}) collective-permute-start(bf16[5,336,128]{2,1,0:T(8,128)(2,1)S(1)} %get-tuple-element.49), channel_id=1, source_target_pairs={{0,4},{2,6},{4,0},{6,2},{8,12},{10,14},{12,8},{14,10},{16,20},{18,... | collective-permute-start | bytes 1290248 | tf_op jit(solution)/shard_map/ppermute | solution.py:325
  84.0 41.8 %collective-permute-start.6 = (bf16[5,336,128]{2,1,0:T(8,128)(2,1)S(1)}, bf16[5,336,128]{2,1,0:T(8,128)(2,1)S(1)}, u32[]{:S(2)}, u32[]{:S(2)}) collective-permute-start(bf16[5,336,128]{2,1,0:T(8,128)(2,1)S(1)} %get-tuple-element.50), channel_id=1, source_target_pairs={{0,6},{2,4},{4,2},{6,0},{8,14},{10,12},{12,10},{14,8},{16,22},{18,... | collective-permute-start | bytes 1290248 | tf_op jit(solution)/shard_map/ppermute | solution.py:325
  126.4 33.6 %collective-permute-start.13 = (bf16[32,5120]{1,0:T(8,128)(2,1)S(1)}, bf16[32,5120]{1,0:T(8,128)(2,1)S(1)}, u32[]{:S(2)}, u32[]{:S(2)}) collective-permute-start(bf16[32,5120]{1,0:T(8,128)(2,1)S(1)} %shard_map.124.refs_9_), channel_id=1, source_target_pairs={{0,1},{1,0},{2,3},{3,2},{4,5},{5,4},{6,7},{7,6},{8,9},{9,8},{10,11... | collective-permute-start | bytes 983048 | tf_op jit(solution)/shard_map/ppermute | solution.py:376
  127.8 13.0 %collective-permute-start.17 = (bf16[216,640]{1,0:T(8,128)(2,1)S(1)}, bf16[216,640]{1,0:T(8,128)(2,1)S(1)}, u32[]{:S(2)}, u32[]{:S(2)}) collective-permute-start(bf16[216,640]{1,0:T(8,128)(2,1)S(1)} %get-tuple-element.65), channel_id=1, source_target_pairs={{0,8},{2,10},{4,12},{6,14},{8,16},{10,18},{12,20},{14,22},{16,24},... | collective-permute-start | bytes 829448 | tf_op jit(solution)/shard_map/ppermute | solution.py:320
  127.9 25.7 %collective-permute-start.18 = (bf16[216,640]{1,0:T(8,128)(2,1)S(1)}, bf16[216,640]{1,0:T(8,128)(2,1)S(1)}, u32[]{:S(2)}, u32[]{:S(2)}) collective-permute-start(bf16[216,640]{1,0:T(8,128)(2,1)S(1)} %get-tuple-element.66), channel_id=1, source_target_pairs={{0,16},{2,18},{4,20},{6,22},{8,24},{10,26},{12,28},{14,30},{16,32}... | collective-permute-start | bytes 829448 | tf_op jit(solution)/shard_map/ppermute | solution.py:320
  130.7 5.7 %collective-permute-start.24 = (f32[32,128]{1,0:T(8,128)S(1)}, f32[32,128]{1,0:T(8,128)S(1)}, u32[]{:S(2)}, u32[]{:S(2)}) collective-permute-start(f32[32,128]{1,0:T(8,128)S(1)} %shard_map.128.mine), channel_id=1, source_target_pairs={{0,1},{1,0},{2,3},{3,2},{4,5},{5,4},{6,7},{7,6},{8,9},{9,8},{10,11... | collective-permute-start | bytes 49160 | tf_op jit(solution)/shard_map/ppermute | solution.py:377
  132.8 38.8 %collective-permute-start.19 = (bf16[216,640]{1,0:T(8,128)(2,1)S(1)}, bf16[216,640]{1,0:T(8,128)(2,1)S(1)}, u32[]{:S(2)}, u32[]{:S(2)}) collective-permute-start(bf16[216,640]{1,0:T(8,128)(2,1)S(1)} %get-tuple-element.67), channel_id=1, source_target_pairs={{0,24},{2,26},{4,28},{6,30},{8,32},{10,34},{12,36},{14,38},{16,40}... | collective-permute-start | bytes 829448 | tf_op jit(solution)/shard_map/ppermute | solution.py:320
  136.4 40.0 %collective-permute-start.20 = (bf16[216,640]{1,0:T(8,128)(2,1)S(1)}, bf16[216,640]{1,0:T(8,128)(2,1)S(1)}, u32[]{:S(2)}, u32[]{:S(2)}) collective-permute-start(bf16[216,640]{1,0:T(8,128)(2,1)S(1)} %get-tuple-element.68), channel_id=1, source_target_pairs={{0,32},{2,34},{4,36},{6,38},{8,40},{10,42},{12,44},{14,46},{16,48}... | collective-permute-start | bytes 829448 | tf_op jit(solution)/shard_map/ppermute | solution.py:320
  140.8 35.6 %collective-permute-start.21 = (bf16[216,640]{1,0:T(8,128)(2,1)S(1)}, bf16[216,640]{1,0:T(8,128)(2,1)S(1)}, u32[]{:S(2)}, u32[]{:S(2)}) collective-permute-start(bf16[216,640]{1,0:T(8,128)(2,1)S(1)} %get-tuple-element.69), channel_id=1, source_target_pairs={{0,40},{2,42},{4,44},{6,46},{8,48},{10,50},{12,52},{14,54},{16,56}... | collective-permute-start | bytes 829448 | tf_op jit(solution)/shard_map/ppermute | solution.py:320
  153.5 26.2 %collective-permute-start.22 = (bf16[216,640]{1,0:T(8,128)(2,1)S(1)}, bf16[216,640]{1,0:T(8,128)(2,1)S(1)}, u32[]{:S(2)}, u32[]{:S(2)}) collective-permute-start(bf16[216,640]{1,0:T(8,128)(2,1)S(1)} %get-tuple-element.70), channel_id=1, source_target_pairs={{0,48},{2,50},{4,52},{6,54},{8,56},{10,58},{12,60},{14,62},{16,0},... | collective-permute-start | bytes 829448 | tf_op jit(solution)/shard_map/ppermute | solution.py:320
  160.0 26.0 %collective-permute-start.23 = (bf16[216,640]{1,0:T(8,128)(2,1)S(1)}, bf16[216,640]{1,0:T(8,128)(2,1)S(1)}, u32[]{:S(2)}, u32[]{:S(2)}) collective-permute-start(bf16[216,640]{1,0:T(8,128)(2,1)S(1)} %get-tuple-element.71), channel_id=1, source_target_pairs={{0,56},{2,58},{4,60},{6,62},{8,0},{10,2},{12,4},{14,6},{16,8},{18,... | collective-permute-start | bytes 829448 | tf_op jit(solution)/shard_map/ppermute | solution.py:320
